TPU v7x, 32 devices: a 4x4x1 block of a 4x4x8 slice. The times are simulated.
32 devices in a mesh: dp: 1 (over z), tp: 4 (over y), pp: 8 (over x, core).
Axes of the slice: x: 4, y: 4, z: 1, core: 2. Of those that a mesh axis runs over, the one named last changes fastest.
The devices are a block of a 4x4x8 slice.
Arguments:
- tokens: int32 [4, 128], P('dp')
- labels: int32 [4, 128], P('dp')
- emb_table: bfloat16 [50304, 768], P('tp')
- w_in: bfloat16 [8, 768, 3072], P('pp', None, 'tp')
- w_out: bfloat16 [8, 3072, 768], P('pp', 'tp')
Outputs:
- output 1: float32 [1], P('dp')
- output 2: float32 [8, 768, 3072], P(('dp', 'pp'), None, 'tp')
- output 3: float32 [8, 3072, 768], P(('dp', 'pp'), 'tp')
- output 4: float32 [50304, 768], P(('dp', 'tp'))
All inputs are finite; a program needn't handle non-finite values.
Results may differ from a plain program's by a relative error of at most 0.0122117.
Values are sent between devices in bfloat16 or wider.
A program may use at most 768 MiB of HBM per device.

v0:
```python
import jax
import jax.numpy as jnp
from jax import lax
from jax.sharding import PartitionSpec as P

NORM_EPS = 1e-6


def contract(lhs, rhs, lhs_dim, rhs_dim):
    return lax.dot_general(lhs, rhs, (((lhs_dim,), (rhs_dim,)), ((), ())), preferred_element_type=jnp.float32)


def solution(mesh):
    pp_size = mesh.shape['pp']
    fwd_perm = [(src_stage, src_stage + 1) for src_stage in range(pp_size - 1)]
    bwd_perm = [(src_stage + 1, src_stage) for src_stage in range(pp_size - 1)]

    def device_fn(tokens, labels, emb_table, w_in, w_out):
        num_micro, seq_len = tokens.shape
        vocab_rows, model_dim = emb_table.shape
        w_one = w_in[0]
        w_two = w_out[0]
        hidden_cols = w_one.shape[1]
        stage_idx = lax.axis_index('pp')
        is_first = stage_idx == 0
        is_last = stage_idx == pp_size - 1
        vocab_base = lax.axis_index('tp') * vocab_rows
        tok_local = tokens - vocab_base
        lab_local = labels - vocab_base
        row_ids = jnp.arange(vocab_rows, dtype=jnp.int32)
        num_ticks = num_micro + pp_size - 1
        act_zero = jnp.zeros((seq_len, model_dim), jnp.bfloat16)

        owned_ids = (tok_local >= 0) & (tok_local < vocab_rows) & is_first
        looked_up = jnp.take(emb_table, jnp.clip(tok_local, 0, vocab_rows - 1), axis=0)
        x_first = lax.psum(jnp.where(owned_ids[:, :, None], looked_up, jnp.zeros_like(looked_up)), 'tp')

        def fwd_tick(x_recv, tick_idx):
            fresh_in = lax.dynamic_index_in_dim(x_first, jnp.minimum(tick_idx, num_micro - 1), 0, keepdims=False)
            x_act = jnp.where(is_first, fresh_in, x_recv)
            hidden = jnp.dot(x_act, w_one, preferred_element_type=jnp.float32)
            gate_act = jax.nn.gelu(hidden).astype(jnp.bfloat16)
            branch_out = lax.psum(jnp.dot(gate_act, w_two, preferred_element_type=jnp.float32), 'tp')
            y_act = (x_act.astype(jnp.float32) + branch_out).astype(jnp.bfloat16)
            return lax.ppermute(y_act, 'pp', fwd_perm), (x_act, hidden, y_act)

        x_hist, h_hist, y_hist = lax.scan(fwd_tick, act_zero, jnp.arange(num_ticks))[1]
        x_saved = lax.dynamic_slice_in_dim(x_hist, stage_idx, num_micro, 0)
        h_saved = lax.dynamic_slice_in_dim(h_hist, stage_idx, num_micro, 0)
        y_top = y_hist[pp_size - 1:]

        def head_step(carry_in, micro_in):
            loss_sum, head_grad = carry_in
            y_act, lab_row = micro_in
            x_wide = y_act.astype(jnp.float32)
            inv_rms = lax.rsqrt(jnp.mean(x_wide * x_wide, axis=-1, keepdims=True) + NORM_EPS)
            normed = x_wide * inv_rms
            normed_b = normed.astype(jnp.bfloat16)
            target_hit = lab_row[:, None] == row_ids[None, :]

            def logit_part():
                logits = contract(normed_b, emb_table, 1, 1)
                local_lse = jax.nn.logsumexp(logits, axis=-1)
                local_target = jnp.sum(jnp.where(target_hit, logits, 0.0), axis=-1)
                return logits, local_lse, local_target

            def logit_skip():
                flat_zero = jnp.zeros((seq_len,), jnp.float32)
                return jnp.zeros((seq_len, vocab_rows), jnp.float32), flat_zero, flat_zero

            logits, local_lse, local_target = lax.cond(is_last, logit_part, logit_skip)
            log_norm = jax.nn.logsumexp(lax.all_gather(local_lse, 'tp'), axis=0)
            target_logit = lax.psum(local_target, 'tp')

            def grad_part():
                grad_logits = (jnp.exp(logits - log_norm[:, None]) - target_hit.astype(jnp.float32)).astype(jnp.bfloat16)
                return head_grad + contract(grad_logits, normed_b, 0, 0), contract(grad_logits, emb_table, 1, 0)

            def grad_skip():
                return head_grad, jnp.zeros((seq_len, model_dim), jnp.float32)

            new_head, normed_part = lax.cond(is_last, grad_part, grad_skip)
            grad_normed = lax.psum(normed_part, 'tp')
            grad_top = (inv_rms * (grad_normed - normed * jnp.mean(normed * grad_normed, axis=-1, keepdims=True))).astype(jnp.bfloat16)
            return (loss_sum + jnp.sum(log_norm - target_logit), new_head), grad_top

        head_init = (jnp.zeros((), jnp.float32), jnp.zeros((vocab_rows, model_dim), jnp.float32))
        head_out, grad_tops = lax.scan(head_step, head_init, (y_top, lab_local))
        loss_sum, head_grad = head_out

        def bwd_tick(carry_in, tick_idx):
            g_recv, acc_one, acc_two, acc_table = carry_in
            micro_idx = tick_idx - (pp_size - 1 - stage_idx)
            is_valid = (micro_idx >= 0) & (micro_idx < num_micro)
            pick_idx = jnp.clip(micro_idx, 0, num_micro - 1)
            top_in = lax.dynamic_index_in_dim(grad_tops, pick_idx, 0, keepdims=False)
            grad_y = jnp.where(is_valid, jnp.where(is_last, top_in, g_recv), act_zero)
            x_act = lax.dynamic_index_in_dim(x_saved, pick_idx, 0, keepdims=False)
            hidden = lax.dynamic_index_in_dim(h_saved, pick_idx, 0, keepdims=False)
            gate_act, gelu_vjp = jax.vjp(jax.nn.gelu, hidden)
            grad_hidden = gelu_vjp(contract(grad_y, w_two, 1, 1))[0].astype(jnp.bfloat16)
            acc_two = acc_two + contract(gate_act.astype(jnp.bfloat16), grad_y, 0, 0)
            acc_one = acc_one + contract(x_act, grad_hidden, 0, 0)
            grad_x = (grad_y.astype(jnp.float32) + lax.psum(contract(grad_hidden, w_one, 1, 1), 'tp')).astype(jnp.bfloat16)
            tok_row = lax.dynamic_index_in_dim(tok_local, pick_idx, 0, keepdims=False)

            def add_rows():
                one_hot = (tok_row[:, None] == row_ids[None, :]).astype(jnp.bfloat16)
                return acc_table + contract(one_hot, grad_x, 0, 0)

            def keep_rows():
                return acc_table

            new_table = lax.cond(is_first, add_rows, keep_rows)
            return (lax.ppermute(grad_x, 'pp', bwd_perm), acc_one, acc_two, new_table), None

        bwd_init = (act_zero, jnp.zeros((model_dim, hidden_cols), jnp.float32), jnp.zeros((hidden_cols, model_dim), jnp.float32), jnp.zeros((vocab_rows, model_dim), jnp.float32))
        bwd_out = lax.scan(bwd_tick, bwd_init, jnp.arange(num_ticks))[0]
        grad_table = lax.psum(bwd_out[3] + head_grad, 'pp')
        mean_loss = lax.psum(jnp.where(is_last, loss_sum, 0.0), 'pp') / (num_micro * seq_len)
        return mean_loss.reshape(1), bwd_out[1][None], bwd_out[2][None], grad_table

    return jax.shard_map(device_fn, mesh=mesh, in_specs=(P('dp', None), P('dp', None), P('tp', None), P('pp', None, 'tp'), P('pp', 'tp', None)), out_specs=(P('dp'), P(('dp', 'pp'), None, 'tp'), P(('dp', 'pp'), 'tp', None), P(('dp', 'tp'), None)), check_vma=False)
```

profile of v0, /device:TPU:97, one launch (start us, length us, event | category | flops | bytes accessed | tf_op | source)
XLA Modules:
  0.0 2482.9 jit_solution(11777343639029303192)
XLA Ops:
  21.3 41.3 %all-reduce.6.cloned.1.call-done = bf16[4,128,768]{2,1,0:T(8,128)(2,1)} async-done(((bf16[4,128,768]{2,1,0:T(8,128)(2,1)}), bf16[4,128,768]{2,1,0:T(8,128)(2,1)}) %all-reduce.6.cloned.1.call-update) | async-done | bytes 786448 | tf_op jit(solution)/shard_map/psum | solution.py:36
  62.7 569.1 %while.59 = (s32[]{:T(128)}, bf16[128,768]{1,0:T(8,128)(2,1)S(1)}, bf16[11,128,768]{2,1,0:T(8,128)(2,1)}, f32[11,128,768]{2,1,0:T(8,128)}, bf16[11,128,768]{2,1,...) while((s32[]{:T(128)}, bf16[128,768]{1,0:T(8,128)(2,1)S(1)}, ...), condition=%wide.region_3.4_spmd.clone, body=%wide.region_1.3_spmd.sunk.clone | while | flops 303366144 | bytes 9046267 | solution.py:47
  67.9 37.8 %all-reduce.10.cloned.1.call-done = f32[128,768]{1,0:T(8,128)} async-done(((f32[128,768]{1,0:T(8,128)}), f32[128,768]{1,0:T(8,128)}) %all-reduce.10.cloned.1.call-update) | async-done | bytes 393232 | tf_op jit(solution)/shard_map/while/body/eval_jaxpr/psum | solution.py:43
  378.9 36.4 %all-reduce.10.cloned.1.call-done = f32[128,768]{1,0:T(8,128)} async-done(((f32[128,768]{1,0:T(8,128)}), f32[128,768]{1,0:T(8,128)}) %all-reduce.10.cloned.1.call-update) | async-done | bytes 393232 | tf_op jit(solution)/shard_map/while/body/eval_jaxpr/psum | solution.py:43
  430.6 36.4 %all-reduce.10.cloned.1.call-done = f32[128,768]{1,0:T(8,128)} async-done(((f32[128,768]{1,0:T(8,128)}), f32[128,768]{1,0:T(8,128)}) %all-reduce.10.cloned.1.call-update) | async-done | bytes 393232 | tf_op jit(solution)/shard_map/while/body/eval_jaxpr/psum | solution.py:43
  650.5 490.6 %while.60 = (s32[]{:T(128)}, f32[]{:T(128)}, f32[12576,768]{1,0:T(8,128)}, bf16[4,128,768]{2,1,0:T(8,128)(2,1)}, pred[]{:T(512)}, /*index=5*/bf16[4,128,768]{2,1...) while((s32[]{:T(128)}, f32[]{:T(128)}, f32[12576,768]{1,0:T(8,128)}, ...), condition=%wide.region_19.20_spmd.clone.clone, body=%wide.region_4.19_spmd.clone.sunk.clone | while | flops 7451495424 | bytes 170901824 | solution.py:88
  669.6 98.4 %all-reduce.12.cloned.1.call-done = f32[128,768]{1,0:T(8,128)} async-done(((f32[128,768]{1,0:T(8,128)}), f32[128,768]{1,0:T(8,128)}) %all-reduce.12.cloned.1.call-update) | async-done | bytes 393232 | tf_op jit(solution)/shard_map/while/body/eval_jaxpr/psum | solution.py:83
  790.1 101.2 %all-reduce.12.cloned.1.call-done = f32[128,768]{1,0:T(8,128)} async-done(((f32[128,768]{1,0:T(8,128)}), f32[128,768]{1,0:T(8,128)}) %all-reduce.12.cloned.1.call-update) | async-done | bytes 393232 | tf_op jit(solution)/shard_map/while/body/eval_jaxpr/psum | solution.py:83
  913.4 101.2 %all-reduce.12.cloned.1.call-done = f32[128,768]{1,0:T(8,128)} async-done(((f32[128,768]{1,0:T(8,128)}), f32[128,768]{1,0:T(8,128)}) %all-reduce.12.cloned.1.call-update) | async-done | bytes 393232 | tf_op jit(solution)/shard_map/while/body/eval_jaxpr/psum | solution.py:83
  1036.8 101.3 %all-reduce.12.cloned.1.call-done = f32[128,768]{1,0:T(8,128)} async-done(((f32[128,768]{1,0:T(8,128)}), f32[128,768]{1,0:T(8,128)}) %all-reduce.12.cloned.1.call-update) | async-done | bytes 393232 | tf_op jit(solution)/shard_map/while/body/eval_jaxpr/psum | solution.py:83
  1154.8 844.9 %while.61 = (s32[]{:T(128)}, bf16[128,768]{1,0:T(8,128)(2,1)}, f32[768,768]{1,0:T(8,128)}, f32[768,768]{1,0:T(8,128)S(1)}, f32[12576,768]{1,0:T(8,128)}, /*index...) while((s32[]{:T(128)}, bf16[128,768]{1,0:T(8,128)(2,1)}, ...), condition=%wide.region_25.26_spmd.clone.clone, body=%wide.region_21.25_spmd.clone.sunk.clone | while | flops 3093590016 | bytes 97817760 | solution.py:118
  1219.7 58.1 %all-reduce.14.cloned.1.call-done = f32[128,768]{1,0:T(8,128)} async-done(((f32[128,768]{1,0:T(8,128)}), f32[128,768]{1,0:T(8,128)}) %all-reduce.14.cloned.1.call-update) | async-done | bytes 393232 | tf_op jit(solution)/shard_map/while/body/eval_jaxpr/psum | solution.py:104
  1297.8 58.9 %all-reduce.14.cloned.1.call-done = f32[128,768]{1,0:T(8,128)} async-done(((f32[128,768]{1,0:T(8,128)}), f32[128,768]{1,0:T(8,128)}) %all-reduce.14.cloned.1.call-update) | async-done | bytes 393232 | tf_op jit(solution)/shard_map/while/body/eval_jaxpr/psum | solution.py:104
  1376.9 58.9 %all-reduce.14.cloned.1.call-done = f32[128,768]{1,0:T(8,128)} async-done(((f32[128,768]{1,0:T(8,128)}), f32[128,768]{1,0:T(8,128)}) %all-reduce.14.cloned.1.call-update) | async-done | bytes 393232 | tf_op jit(solution)/shard_map/while/body/eval_jaxpr/psum | solution.py:104
  1455.9 58.9 %all-reduce.14.cloned.1.call-done = f32[128,768]{1,0:T(8,128)} async-done(((f32[128,768]{1,0:T(8,128)}), f32[128,768]{1,0:T(8,128)}) %all-reduce.14.cloned.1.call-update) | async-done | bytes 393232 | tf_op jit(solution)/shard_map/while/body/eval_jaxpr/psum | solution.py:104
  1534.9 58.9 %all-reduce.14.cloned.1.call-done = f32[128,768]{1,0:T(8,128)} async-done(((f32[128,768]{1,0:T(8,128)}), f32[128,768]{1,0:T(8,128)}) %all-reduce.14.cloned.1.call-update) | async-done | bytes 393232 | tf_op jit(solution)/shard_map/while/body/eval_jaxpr/psum | solution.py:104
  1613.9 58.9 %all-reduce.14.cloned.1.call-done = f32[128,768]{1,0:T(8,128)} async-done(((f32[128,768]{1,0:T(8,128)}), f32[128,768]{1,0:T(8,128)}) %all-reduce.14.cloned.1.call-update) | async-done | bytes 393232 | tf_op jit(solution)/shard_map/while/body/eval_jaxpr/psum | solution.py:104
  1692.9 58.9 %all-reduce.14.cloned.1.call-done = f32[128,768]{1,0:T(8,128)} async-done(((f32[128,768]{1,0:T(8,128)}), f32[128,768]{1,0:T(8,128)}) %all-reduce.14.cloned.1.call-update) | async-done | bytes 393232 | tf_op jit(solution)/shard_map/while/body/eval_jaxpr/psum | solution.py:104
  1771.9 58.9 %all-reduce.14.cloned.1.call-done = f32[128,768]{1,0:T(8,128)} async-done(((f32[128,768]{1,0:T(8,128)}), f32[128,768]{1,0:T(8,128)}) %all-reduce.14.cloned.1.call-update) | async-done | bytes 393232 | tf_op jit(solution)/shard_map/while/body/eval_jaxpr/psum | solution.py:104
  1850.9 58.9 %all-reduce.14.cloned.1.call-done = f32[128,768]{1,0:T(8,128)} async-done(((f32[128,768]{1,0:T(8,128)}), f32[128,768]{1,0:T(8,128)}) %all-reduce.14.cloned.1.call-update) | async-done | bytes 393232 | tf_op jit(solution)/shard_map/while/body/eval_jaxpr/psum | solution.py:104
  1929.9 58.9 %all-reduce.14.cloned.1.call-done = f32[128,768]{1,0:T(8,128)} async-done(((f32[128,768]{1,0:T(8,128)}), f32[128,768]{1,0:T(8,128)}) %all-reduce.14.cloned.1.call-update) | async-done | bytes 393232 | tf_op jit(solution)/shard_map/while/body/eval_jaxpr/psum | solution.py:104
  1999.8 39.3 %add.115 = f32[12576,768]{1,0:T(8,128)} add(f32[12576,768]{1,0:T(8,128)} %get-tuple-element.383, f32[12576,768]{1,0:T(8,128)} %get-tuple-element.384) | non-fusion elementwise | flops 9658368 | bytes 115900416 | tf_op jit(solution)/shard_map/add | solution.py:119
  2039.1 40.8 %psum.53 = f32[]{:T(128)} all-reduce(f32[]{:T(128)S(6)} %select_n.84), channel_id=1, replica_groups=mesh['dp'=1,'tp'=4,'pp'=8] {'pp'}, use_global_device_ids=true, to_apply=%region_20.21 | all-reduce | flops 1 | bytes 8 | tf_op jit(solution)/shard_map/psum | solution.py:120
  2080.6 367.0 %all-reduce.8.cloned.1.call-done = f32[12576,768]{1,0:T(8,128)} async-done(((f32[12576,768]{1,0:T(8,128)}), f32[12576,768]{1,0:T(8,128)}) %all-reduce.8.cloned.1.call-update) | async-done | bytes 38633488 | tf_op jit(solution)/shard_map/psum | solution.py:119
  (432 shorter events, 871.6 us)
Async XLA Ops:
  7.2 55.5 %all-reduce.6.cloned.1.call-start = ((), (), s32[]{:S(2)}) async-start(), calls=%async_computation | async-start | bytes 1572864 | tf_op jit(solution)/shard_map/psum | solution.py:36
  62.7 43.0 %all-reduce.10.cloned.1.call-start = ((), (), s32[]{:S(2)}) async-start(), calls=%async_computation.2 | async-start | bytes 786432 | tf_op jit(solution)/shard_map/while/body/eval_jaxpr/psum | solution.py:43
  115.8 41.5 %all-reduce.10.cloned.1.call-start = ((), (), s32[]{:S(2)}) async-start(), calls=%async_computation.2 | async-start | bytes 786432 | tf_op jit(solution)/shard_map/while/body/eval_jaxpr/psum | solution.py:43
  219.0 41.5 %all-reduce.10.cloned.1.call-start = ((), (), s32[]{:S(2)}) async-start(), calls=%async_computation.2 | async-start | bytes 786432 | tf_op jit(solution)/shard_map/while/body/eval_jaxpr/psum | solution.py:43
  270.6 41.5 %all-reduce.10.cloned.1.call-start = ((), (), s32[]{:S(2)}) async-start(), calls=%async_computation.2 | async-start | bytes 786432 | tf_op jit(solution)/shard_map/while/body/eval_jaxpr/psum | solution.py:43
  322.2 41.5 %all-reduce.10.cloned.1.call-start = ((), (), s32[]{:S(2)}) async-start(), calls=%async_computation.2 | async-start | bytes 786432 | tf_op jit(solution)/shard_map/while/body/eval_jaxpr/psum | solution.py:43
  373.8 41.6 %all-reduce.10.cloned.1.call-start = ((), (), s32[]{:S(2)}) async-start(), calls=%async_computation.2 | async-start | bytes 786432 | tf_op jit(solution)/shard_map/while/body/eval_jaxpr/psum | solution.py:43
  425.4 41.5 %all-reduce.10.cloned.1.call-start = ((), (), s32[]{:S(2)}) async-start(), calls=%async_computation.2 | async-start | bytes 786432 | tf_op jit(solution)/shard_map/while/body/eval_jaxpr/psum | solution.py:43
  650.5 117.5 %all-reduce.12.cloned.1.call-start = ((), (), s32[]{:S(2)}) async-start(), calls=%async_computation.3 | async-start | bytes 786432 | tf_op jit(solution)/shard_map/while/body/eval_jaxpr/psum | solution.py:83
  771.0 120.3 %all-reduce.12.cloned.1.call-start = ((), (), s32[]{:S(2)}) async-start(), calls=%async_computation.3 | async-start | bytes 786432 | tf_op jit(solution)/shard_map/while/body/eval_jaxpr/psum | solution.py:83
  894.4 120.3 %all-reduce.12.cloned.1.call-start = ((), (), s32[]{:S(2)}) async-start(), calls=%async_computation.3 | async-start | bytes 786432 | tf_op jit(solution)/shard_map/while/body/eval_jaxpr/psum | solution.py:83
  1017.7 120.3 %all-reduce.12.cloned.1.call-start = ((), (), s32[]{:S(2)}) async-start(), calls=%async_computation.3 | async-start | bytes 786432 | tf_op jit(solution)/shard_map/while/body/eval_jaxpr/psum | solution.py:83
  1154.8 44.8 %all-reduce.14.cloned.1.call-start = ((), (), s32[]{:S(2)}) async-start(), calls=%async_computation.4 | async-start | bytes 786432 | tf_op jit(solution)/shard_map/while/body/eval_jaxpr/psum | solution.py:104
  1210.5 67.3 %all-reduce.14.cloned.1.call-start = ((), (), s32[]{:S(2)}) async-start(), calls=%async_computation.4 | async-start | bytes 786432 | tf_op jit(solution)/shard_map/while/body/eval_jaxpr/psum | solution.py:104
  1288.7 68.1 %all-reduce.14.cloned.1.call-start = ((), (), s32[]{:S(2)}) async-start(), calls=%async_computation.4 | async-start | bytes 786432 | tf_op jit(solution)/shard_map/while/body/eval_jaxpr/psum | solution.py:104
  1367.7 68.1 %all-reduce.14.cloned.1.call-start = ((), (), s32[]{:S(2)}) async-start(), calls=%async_computation.4 | async-start | bytes 786432 | tf_op jit(solution)/shard_map/while/body/eval_jaxpr/psum | solution.py:104
  1446.7 68.1 %all-reduce.14.cloned.1.call-start = ((), (), s32[]{:S(2)}) async-start(), calls=%async_computation.4 | async-start | bytes 786432 | tf_op jit(solution)/shard_map/while/body/eval_jaxpr/psum | solution.py:104
  1525.7 68.1 %all-reduce.14.cloned.1.call-start = ((), (), s32[]{:S(2)}) async-start(), calls=%async_computation.4 | async-start | bytes 786432 | tf_op jit(solution)/shard_map/while/body/eval_jaxpr/psum | solution.py:104
  1604.7 68.1 %all-reduce.14.cloned.1.call-start = ((), (), s32[]{:S(2)}) async-start(), calls=%async_computation.4 | async-start | bytes 786432 | tf_op jit(solution)/shard_map/while/body/eval_jaxpr/psum | solution.py:104
  1683.7 68.1 %all-reduce.14.cloned.1.call-start = ((), (), s32[]{:S(2)}) async-start(), calls=%async_computation.4 | async-start | bytes 786432 | tf_op jit(solution)/shard_map/while/body/eval_jaxpr/psum | solution.py:104
  1762.7 68.1 %all-reduce.14.cloned.1.call-start = ((), (), s32[]{:S(2)}) async-start(), calls=%async_computation.4 | async-start | bytes 786432 | tf_op jit(solution)/shard_map/while/body/eval_jaxpr/psum | solution.py:104
  1841.7 68.1 %all-reduce.14.cloned.1.call-start = ((), (), s32[]{:S(2)}) async-start(), calls=%async_computation.4 | async-start | bytes 786432 | tf_op jit(solution)/shard_map/while/body/eval_jaxpr/psum | solution.py:104
  1920.7 68.1 %all-reduce.14.cloned.1.call-start = ((), (), s32[]{:S(2)}) async-start(), calls=%async_computation.4 | async-start | bytes 786432 | tf_op jit(solution)/shard_map/while/body/eval_jaxpr/psum | solution.py:104
  1999.7 447.9 %all-reduce.8.cloned.1.call-start = ((), (), s32[]{:S(2)}) async-start(), calls=%async_computation.1 | async-start | bytes 77266944 | tf_op jit(solution)/shard_map/psum | solution.py:119
  (59 other events, 563.5 us)
Sparse Core Ops, SparseCore 0:
  21.4 41.2 all-reduce.5
  68.0 37.6 all-reduce.9
  224.2 36.2 all-reduce.9
  327.4 36.2 all-reduce.9
  379.0 36.2 all-reduce.9
  430.7 36.2 all-reduce.9
  482.3 36.2 all-reduce.9
  533.9 36.2 all-reduce.9
  669.1 98.8 all-reduce.11
  789.6 101.7 all-reduce.11
  912.9 101.7 all-reduce.11
  1036.3 101.7 all-reduce.11
  1162.0 37.6 all-reduce.13
  1217.6 60.1 all-reduce.13
  1295.8 60.9 all-reduce.13
  1374.8 60.9 all-reduce.13
  1453.8 60.9 all-reduce.13
  1532.8 60.9 all-reduce.13
  1611.8 60.9 all-reduce.13
  1690.8 60.9 all-reduce.13
  1769.8 60.9 all-reduce.13
  1848.8 60.9 all-reduce.13
  1927.8 60.9 all-reduce.13
  2039.3 408.3 all-reduce.7
  (4 shorter events, 144.8 us)
where the time goes:
time: 2490 us; the launch traced here: 2480 us
  waiting for transfers between devices  1870 us (75%)
  other arithmetic  129 us (5%)
  matrix products  125 us (5%)
  local copies, waits for them, and re-layouts  121 us (5%)
  starting transfers between devices  116 us (5%)
  blocking collectives  91.7 us (4%)
    psum x11, waiting for transfers between devices, bwd_tick(): lax.psum(contract(grad_hidden, w_one, 1, 1), 'tp')  624 us
    psum x4, waiting for transfers between devices, head_step(): grad_normed = lax.psum(normed_part, 'tp')  402 us
    psum x11, waiting for transfers between devices, fwd_tick(): lax.psum(jnp.dot(gate_act, w_two, preferred_element_type=jnp.float32), 'tp')  402 us
    psum x1, waiting for transfers between devices, device_fn(): grad_table = lax.psum(bwd_out[3] + head_grad, 'pp')  367 us
    dot_general x44, matrix products, contract(): lax.dot_general(lhs, rhs, (((lhs_dim,), (rhs_dim,)), ((), ())), preferred...  101 us
    ppermute x11, starting transfers between devices, fwd_tick(): return (lax.ppermute(y_act, 'pp', fwd_perm), (x_act, hidden, y_act))  63.6 us
    ppermute x11, starting transfers between devices, bwd_tick(): lax.ppermute(grad_x, 'pp', bwd_perm)  51.8 us
  transfers between devices with their start and end apart: 50, of which 40 were waited for; matrix products, arithmetic and copies ran while one was open for 3% of the time, Pallas kernels for 0%

commit v1 on v0

v1 whole, which is shorter than its diff:
```python
import jax
import jax.numpy as jnp
from jax import lax
from jax.sharding import PartitionSpec as P

NORM_EPS = 1e-6


def contract(lhs, rhs, lhs_dim, rhs_dim):
    return lax.dot_general(lhs, rhs, (((lhs_dim,), (rhs_dim,)), ((), ())), preferred_element_type=jnp.float32)


def solution(mesh):
    pp_size = mesh.shape['pp']
    fwd_perm = [(src_stage, src_stage + 1) for src_stage in range(pp_size - 1)]
    bwd_perm = [(src_stage + 1, src_stage) for src_stage in range(pp_size - 1)]

    def device_fn(tokens, labels, emb_table, w_in, w_out):
        num_micro, seq_len = tokens.shape
        vocab_rows, model_dim = emb_table.shape
        num_tok = num_micro * seq_len
        stage_idx = lax.axis_index('pp')
        is_first = stage_idx == 0
        is_last = stage_idx == pp_size - 1
        vocab_base = lax.axis_index('tp') * vocab_rows
        tok_local = tokens - vocab_base
        lab_local = (labels - vocab_base).reshape(num_tok)
        row_ids = jnp.arange(vocab_rows, dtype=jnp.int32)

        w_one = lax.all_gather(w_in[0], 'tp', axis=1, tiled=True)
        w_two = lax.all_gather(w_out[0], 'tp', axis=0, tiled=True)

        owned_ids = (tok_local >= 0) & (tok_local < vocab_rows)
        looked_up = jnp.take(emb_table, jnp.clip(tok_local, 0, vocab_rows - 1), axis=0)
        x_act = lax.psum_scatter(jnp.where(owned_ids[:, :, None], looked_up, jnp.zeros_like(looked_up)), 'tp', scatter_dimension=0)

        x_saved = x_act
        hidden = None
        for tick in range(pp_size):
            x_saved = jnp.where(stage_idx == tick, x_act, x_saved)
            hid = jnp.dot(x_act, w_one, preferred_element_type=jnp.float32)
            branch_out = jnp.dot(jax.nn.gelu(hid).astype(jnp.bfloat16), w_two, preferred_element_type=jnp.float32)
            y_act = (x_act.astype(jnp.float32) + branch_out).astype(jnp.bfloat16)
            if tick < pp_size - 1:
                x_act = lax.ppermute(y_act, 'pp', fwd_perm)
        y_top = lax.psum(jnp.where(is_last, y_act, jnp.zeros_like(y_act)), 'pp')
        hidden = jnp.dot(x_saved, w_one, preferred_element_type=jnp.float32)
        gate_act, gelu_vjp = jax.vjp(jax.nn.gelu, hidden)
        gate_act = gate_act.astype(jnp.bfloat16)
        hidden_cols = w_in.shape[2]

        def to_columns(part):
            part = part.reshape(seq_len, num_micro, hidden_cols)
            return lax.all_to_all(part, 'tp', split_axis=1, concat_axis=0, tiled=True).reshape(num_tok, hidden_cols)

        x_all = lax.all_gather(x_saved, 'tp', axis=0, tiled=True)
        gate_cols = to_columns(gate_act)

        x_wide = y_top.astype(jnp.float32)
        inv_rms = lax.rsqrt(jnp.mean(x_wide * x_wide, axis=-1, keepdims=True) + NORM_EPS)
        normed = x_wide * inv_rms
        normed_all = lax.all_gather(normed.astype(jnp.bfloat16), 'tp', axis=0, tiled=True)

        target_hit = lab_local[:, None] == row_ids[None, :]
        logits = contract(normed_all, emb_table, 1, 1)
        local_max = jnp.max(logits, axis=-1)
        local_sum = jnp.sum(jnp.exp(logits - local_max[:, None]), axis=-1)
        local_target = jnp.sum(jnp.where(target_hit, logits, 0.0), axis=-1)
        stats = lax.all_gather(jnp.stack([local_max + jnp.log(local_sum), local_target]), 'tp')
        log_norm = jax.nn.logsumexp(stats[:, 0], axis=0)
        target_logit = jnp.sum(stats[:, 1], axis=0)
        loss_sum = jnp.sum(log_norm - target_logit)
        grad_logits = (jnp.exp(logits - log_norm[:, None]) - target_hit.astype(jnp.float32)).astype(jnp.bfloat16)
        grad_normed = lax.psum_scatter(contract(grad_logits, emb_table, 1, 0), 'tp', scatter_dimension=0, tiled=True)
        grad_y = (inv_rms * (grad_normed - normed * jnp.mean(normed * grad_normed, axis=-1, keepdims=True))).astype(jnp.bfloat16)

        dy_saved = grad_y
        for tick in range(pp_size):
            here = stage_idx == pp_size - 1 - tick
            dy_saved = jnp.where(here, grad_y, dy_saved)
            grad_hidden = gelu_vjp(contract(grad_y, w_two, 1, 1))[0].astype(jnp.bfloat16)
            dh_saved = grad_hidden if tick == 0 else jnp.where(here, grad_hidden, dh_saved)
            grad_x = (grad_y.astype(jnp.float32) + contract(grad_hidden, w_one, 1, 1)).astype(jnp.bfloat16)
            if tick < pp_size - 1:
                grad_y = lax.ppermute(grad_x, 'pp', bwd_perm)
        dx_all = lax.all_gather(lax.psum(jnp.where(is_first, grad_x, jnp.zeros_like(grad_x)), 'pp'), 'tp', axis=0, tiled=True)
        dy_all = lax.all_gather(dy_saved, 'tp', axis=0, tiled=True)
        dh_cols = to_columns(dh_saved)
        grad_two = contract(gate_cols, dy_all, 0, 0)
        grad_one = contract(x_all, dh_cols, 0, 0)

        one_hot = (tok_local.reshape(num_tok)[:, None] == row_ids[None, :]).astype(jnp.bfloat16)
        grad_table = contract(grad_logits, normed_all, 0, 0) + contract(one_hot, dx_all, 0, 0)
        mean_loss = loss_sum / num_tok
        return mean_loss.reshape(1), grad_one[None], grad_two[None], grad_table

    return jax.shard_map(device_fn, mesh=mesh, in_specs=(P('dp', None), P('dp', None), P('tp', None), P('pp', None, 'tp'), P('pp', 'tp', None)), out_specs=(P('dp'), P(('dp', 'pp'), None, 'tp'), P(('dp', 'pp'), 'tp', None), P(('dp', 'tp'), None)), check_vma=False)
```

time: 2490 us -> 659 us (0.26)
  the two profiles are of different devices: /device:TPU:97 before, /device:TPU:96 now
where the time goes in v1:
time: 659 us; the launch traced here: 650 us
  waiting for transfers between devices  272 us (41%)
  matrix products  203 us (31%)
  blocking collectives  70.2 us (11%)
  starting transfers between devices  54.6 us (8%)
  other arithmetic  20.1 us (3%)
  between operations  17 us (3%)
  local copies, waits for them, and re-layouts  14.2 us (2%)
    dot_general x22, matrix products, contract(): lax.dot_general(lhs, rhs, (((lhs_dim,), (rhs_dim,)), ((), ())), preferred...  153 us
    psum x1, waiting for transfers between devices, device_fn(): y_top = lax.psum(jnp.where(is_last, y_act, jnp.zeros_like(y_act)), 'pp')  60.5 us
    all_gather x1, waiting for transfers between devices, device_fn(): w_one = lax.all_gather(w_in[0], 'tp', axis=1, tiled=True)  52 us
    all_gather x1, waiting for transfers between devices, device_fn(): w_two = lax.all_gather(w_out[0], 'tp', axis=0, tiled=True)  51.2 us
    dot_general x8, matrix products, device_fn(): jnp.dot(jax.nn.gelu(hid).astype(jnp.bfloat16), w_two, preferred_element_t...  44.5 us
    psum x1, waiting for transfers between devices, device_fn(): lax.psum(jnp.where(is_first, grad_x, jnp.zeros_like(grad_x)), 'pp')  43 us
    ppermute x7, starting transfers between devices, device_fn(): x_act = lax.ppermute(y_act, 'pp', fwd_perm)  37.1 us
    reduce_scatter x1, waiting for transfers between devices, device_fn(): lax.psum_scatter(jnp.where(owned_ids[:, :, None], looked_up, jnp.zeros_li...  21.3 us
  transfers between devices with their start and end apart: 22, of which 18 were waited for; matrix products, arithmetic and copies ran while one was open for 14% of the time, Pallas kernels for 0%

profile of v1, /device:TPU:96, one launch (start us, length us, event | category | flops | bytes accessed | tf_op | source)
XLA Modules:
  0.0 650.3 jit_solution(7370687784594027545)
XLA Ops:
  9.2 11.4 %gather_fusion = bf16[512,768]{1,0:T(8,128)(2,1)S(1)} fusion(bf16[12576,768]{1,0:T(8,128)(2,1)} %param.7, s32[1024]{0:T(1024)S(1)} %pad_clamp_fusion), kind=kCustom, calls=%fused_computation | custom fusion | bytes 1574912 | tf_op jit(solution)/shard_map/jit(_take)/gather | solution.py:34
  23.4 21.3 %reduce-scatter.3.cloned.1.call-done = bf16[1,128,768]{2,1,0:T(8,128)(2,1)} async-done(((bf16[4,128,768]{2,1,0:T(8,128)(2,1)}), bf16[1,128,768]{2,1,0:T(8,128)(2,1)}) %reduce-scatter.3.cloned.1.call-update) | async-done | bytes 196624 | tf_op jit(solution)/shard_map/reduce_scatter | solution.py:35
  44.7 51.2 %all-gather.9.cloned.1.call-done = bf16[1,3072,768]{2,1,0:T(8,128)(2,1)} async-done(((bf16[1,768,768]{2,1,0:T(8,128)(2,1)}), bf16[1,3072,768]{2,1,0:T(8,128)(2,1)}) %all-gather.9.cloned.1.call-update) | async-done | bytes 4718608 | tf_op jit(solution)/shard_map/all_gather | solution.py:31
  96.0 52.0 %all-gather.7.cloned.1.call-done = bf16[1,768,3072]{2,1,0:T(8,128)(2,1)} async-done(((bf16[1,768,768]{2,1,0:T(8,128)(2,1)}), bf16[1,768,3072]{2,1,0:T(8,128)(2,1)}) %all-gather.7.cloned.1.call-update) | async-done | bytes 4718608 | tf_op jit(solution)/shard_map/all_gather | solution.py:30
  173.6 6.0 collective-permute-start.2
  186.1 6.2 collective-permute-start.3
  198.6 6.0 collective-permute-start.4
  211.1 6.0 collective-permute-start.5
  223.6 6.0 collective-permute-start.6
  230.6 6.2 fusion.223
  236.9 60.5 %all-reduce.3.cloned.1.call-done = bf16[128,768]{1,0:T(8,128)(2,1)} async-done(((bf16[128,768]{1,0:T(8,128)(2,1)}), bf16[128,768]{1,0:T(8,128)(2,1)}) %all-reduce.3.cloned.1.call-update) | async-done | bytes 196624 | tf_op jit(solution)/shard_map/psum | solution.py:46
  299.4 14.8 %all_gather.26 = bf16[512,768]{1,0:T(8,128)(2,1)S(1)} all-gather(bf16[128,768]{1,0:T(8,128)(2,1)S(1)} %fusion.215), channel_id=1, replica_groups=mesh['dp'=1,'tp'=4,'pp'=8] {'tp'}, dimensions={0}, use_global_device_ids=true | all-gather | bytes 983040 | tf_op jit(solution)/shard_map/all_gather | solution.py:62
  314.2 21.7 %fusion.296 = (f32[512]{0:T(512)S(1)}, f32[512,12576]{0,1:T(8,128)}) fusion(bf16[512,768]{1,0:T(8,128)(2,1)S(1)} %all_gather.26, bf16[12576,768]{1,0:T(8,128)(2,1)} %param.7), kind=kOutput, calls=%fused_computation.262 | convolution fusion | flops 9896607744 | bytes 45860864 | tf_op jit(solution)/shard_map/dot_general | solution.py:10
  335.9 11.8 %exponential_reduce_fusion = (f32[512]{0:T(512)S(1)}, f32[512]{0:T(512)S(1)}) fusion(f32[512,12576]{0,1:T(8,128)} %get-tuple-element.18, f32[512]{0:T(512)S(1)} %get-tuple-element.17, s32[512]{0:T(512)S(1)} %subtract_bitcast_fusion), kind=kLoop, calls=%fused_computation.6 | loop fusion | flops 32193536 | bytes 25763840 | tf_op jit(solution)/shard_map/reduce_sum | solution.py:67
  347.7 12.3 %all-gather.3 = f32[4,2,512]{2,1,0:T(2,128)S(1)} all-gather(f32[1,2,512]{2,1,0:T(2,128)S(1)} %maximum_bitcast_fusion), channel_id=4, replica_groups=mesh['dp'=1,'tp'=4,'pp'=8] {'tp'}, dimensions={0}, use_global_device_ids=true | all-gather | bytes 20480 | tf_op jit(solution)/shard_map/all_gather | solution.py:69
  360.7 21.8 %fusion.222 = f32[512,768]{1,0:T(8,128)} fusion(bf16[12576,768]{1,0:T(8,128)(2,1)} %param.7, f32[512,12576]{0,1:T(8,128)} %get-tuple-element.18, f32[512]{0:T(512)S(1)} %get-tuple-element.9, s32[512]{0:T(512)S(1)} %subtract_bitcast_fusion), kind=kOutput, calls=%fused_computation.199 | convolution fusion | flops 9922363392 | bytes 46649344 | tf_op jit(solution)/shard_map/dot_general | solution.py:10
  388.2 15.8 %reduce-scatter.5.cloned.1.call-done = f32[128,768]{1,0:T(8,128)} async-done(((f32[512,768]{1,0:T(8,128)}), f32[128,768]{1,0:T(8,128)}) %reduce-scatter.5.cloned.1.call-update) | async-done | bytes 393232 | tf_op jit(solution)/shard_map/reduce_scatter | solution.py:74
  433.7 5.7 collective-permute-done.9
  471.0 14.1 %all_gather.29 = bf16[512,768]{1,0:T(8,128)(2,1)} all-gather(bf16[128,768]{1,0:T(8,128)(2,1)S(1)} %fusion.232), channel_id=1, replica_groups=mesh['dp'=1,'tp'=4,'pp'=8] {'tp'}, dimensions={0}, use_global_device_ids=true | all-gather | bytes 983040 | tf_op jit(solution)/shard_map/all_gather | solution.py:56
  492.5 26.6 %fusion.221 = f32[12576,768]{1,0:T(8,128)} fusion(bf16[512,768]{1,0:T(8,128)(2,1)S(1)} %all_gather.26, f32[512,12576]{0,1:T(8,128)} %get-tuple-element.18, f32[512]{0:T(512)S(1)} %get-tuple-element.9, s32[512]{0:T(512)S(1)} %subtract_bitcast_fusion), kind=kOutput, calls=%fused_computation.198 | convolution fusion | flops 9922363392 | bytes 65179648 | tf_op jit(solution)/shard_map/dot_general | solution.py:10
  531.2 14.1 %all_gather.30 = bf16[512,768]{1,0:T(8,128)(2,1)S(1)} all-gather(bf16[128,768]{1,0:T(8,128)(2,1)S(1)} %get-tuple-element.11), channel_id=1, replica_groups=mesh['dp'=1,'tp'=4,'pp'=8] {'tp'}, dimensions={0}, use_global_device_ids=true | all-gather | bytes 983040 | tf_op jit(solution)/shard_map/all_gather | solution.py:87
  551.4 43.0 %all-reduce.5.cloned.1.call-done = bf16[128,768]{1,0:T(8,128)(2,1)} async-done(((bf16[128,768]{1,0:T(8,128)(2,1)}), bf16[128,768]{1,0:T(8,128)(2,1)}) %all-reduce.5.cloned.1.call-update) | async-done | bytes 196624 | tf_op jit(solution)/shard_map/psum | solution.py:86
  594.4 15.0 %all_gather.31 = bf16[512,768]{1,0:T(8,128)(2,1)S(1)} all-gather(bf16[128,768]{1,0:T(8,128)(2,1)} %all-reduce.5.cloned.1.call-done), channel_id=1, replica_groups=mesh['dp'=1,'tp'=4,'pp'=8] {'tp'}, dimensions={0}, use_global_device_ids=true | all-gather | bytes 983040 | tf_op jit(solution)/shard_map/all_gather | solution.py:86
  609.4 30.2 %fusion.1 = f32[12576,768]{1,0:T(8,128)} fusion(f32[12576,768]{1,0:T(8,128)} %fusion.221, bf16[512,768]{1,0:T(8,128)(2,1)S(1)} %all_gather.31, s32[512]{0:T(512)S(1)} %copy-done.10), kind=kOutput, calls=%fused_computation.7 | convolution fusion | flops 9906266112 | bytes 78055424 | tf_op jit(solution)/shard_map/dot_general | solution.py:10
  (127 shorter events, 153.9 us)
Async XLA Ops:
  7.2 37.6 %reduce-scatter.3.cloned.1.call-start = ((), (), s32[]{:S(2)}) async-start(), calls=%async_computation.4 | async-start | bytes 983040 | tf_op jit(solution)/shard_map/reduce_scatter | solution.py:35
  21.8 74.2 %all-gather.9.cloned.1.call-start = ((), (), s32[]{:S(2)}) async-start(), calls=%async_computation.9 | async-start | bytes 5898240 | tf_op jit(solution)/shard_map/all_gather | solution.py:31
  22.6 125.4 %all-gather.7.cloned.1.call-start = ((), (), s32[]{:S(2)}) async-start(), calls=%async_computation.8 | async-start | bytes 5898240 | tf_op jit(solution)/shard_map/all_gather | solution.py:30
  23.4 274.0 %all-reduce.3.cloned.1.call-start = ((), (), s32[]{:S(2)}) async-start(), calls=%async_computation.5 | async-start | bytes 393216 | tf_op jit(solution)/shard_map/psum | solution.py:46
  153.5 2.6 collective-permute-start
  161.6 6.5 %collective-permute-start.1 = (bf16[128,768]{1,0:T(8,128)(2,1)S(1)}, bf16[128,768]{1,0:T(8,128)(2,1)S(1)}, u32[]{:S(2)}, u32[]{:S(2)}) collective-permute-start(bf16[128,768]{1,0:T(8,128)(2,1)S(1)} %add_convert_fusion.21), channel_id=1, source_target_pairs={{0,1},{1,2},{2,3},{3,4},{4,5},{5,6},{6,7},{8,9},{9,10},{10,11},{11... | collective-permute-start | bytes 589832 | tf_op jit(solution)/shard_map/ppermute | solution.py:45
  173.6 7.0 %collective-permute-start.2 = (bf16[128,768]{1,0:T(8,128)(2,1)S(1)}, bf16[128,768]{1,0:T(8,128)(2,1)S(1)}, u32[]{:S(2)}, u32[]{:S(2)}) collective-permute-start(bf16[128,768]{1,0:T(8,128)(2,1)S(1)} %add_convert_fusion.20), channel_id=1, source_target_pairs={{0,1},{1,2},{2,3},{3,4},{4,5},{5,6},{6,7},{8,9},{9,10},{10,11},{11... | collective-permute-start | bytes 589832 | tf_op jit(solution)/shard_map/ppermute | solution.py:45
  186.1 7.0 %collective-permute-start.3 = (bf16[128,768]{1,0:T(8,128)(2,1)S(1)}, bf16[128,768]{1,0:T(8,128)(2,1)S(1)}, u32[]{:S(2)}, u32[]{:S(2)}) collective-permute-start(bf16[128,768]{1,0:T(8,128)(2,1)S(1)} %add_convert_fusion.19), channel_id=1, source_target_pairs={{0,1},{1,2},{2,3},{3,4},{4,5},{5,6},{6,7},{8,9},{9,10},{10,11},{11... | collective-permute-start | bytes 589832 | tf_op jit(solution)/shard_map/ppermute | solution.py:45
  198.6 7.0 %collective-permute-start.4 = (bf16[128,768]{1,0:T(8,128)(2,1)S(1)}, bf16[128,768]{1,0:T(8,128)(2,1)S(1)}, u32[]{:S(2)}, u32[]{:S(2)}) collective-permute-start(bf16[128,768]{1,0:T(8,128)(2,1)S(1)} %add_convert_fusion.18), channel_id=1, source_target_pairs={{0,1},{1,2},{2,3},{3,4},{4,5},{5,6},{6,7},{8,9},{9,10},{10,11},{11... | collective-permute-start | bytes 589832 | tf_op jit(solution)/shard_map/ppermute | solution.py:45
  211.1 7.0 %collective-permute-start.5 = (bf16[128,768]{1,0:T(8,128)(2,1)S(1)}, bf16[128,768]{1,0:T(8,128)(2,1)S(1)}, u32[]{:S(2)}, u32[]{:S(2)}) collective-permute-start(bf16[128,768]{1,0:T(8,128)(2,1)S(1)} %add_convert_fusion.17), channel_id=1, source_target_pairs={{0,1},{1,2},{2,3},{3,4},{4,5},{5,6},{6,7},{8,9},{9,10},{10,11},{11... | collective-permute-start | bytes 589832 | tf_op jit(solution)/shard_map/ppermute | solution.py:45
  223.6 7.0 %collective-permute-start.6 = (bf16[128,768]{1,0:T(8,128)(2,1)S(1)}, bf16[128,768]{1,0:T(8,128)(2,1)S(1)}, u32[]{:S(2)}, u32[]{:S(2)}) collective-permute-start(bf16[128,768]{1,0:T(8,128)(2,1)S(1)} %add_convert_fusion.16), channel_id=1, source_target_pairs={{0,1},{1,2},{2,3},{3,4},{4,5},{5,6},{6,7},{8,9},{9,10},{10,11},{11... | collective-permute-start | bytes 589832 | tf_op jit(solution)/shard_map/ppermute | solution.py:45
  236.8 167.1 %reduce-scatter.5.cloned.1.call-start = ((), (), s32[]{:S(2)}) async-start(), calls=%async_computation.6 | async-start | bytes 1966080 | tf_op jit(solution)/shard_map/reduce_scatter | solution.py:74
  413.0 3.5 collective-permute-start.7
  422.4 6.4 collective-permute-start.8
  432.4 7.0 %collective-permute-start.9 = (bf16[128,768]{1,0:T(8,128)(2,1)S(1)}, bf16[128,768]{1,0:T(8,128)(2,1)S(1)}, u32[]{:S(2)}, u32[]{:S(2)}) collective-permute-start(bf16[128,768]{1,0:T(8,128)(2,1)S(1)} %add_convert_fusion.13), channel_id=1, source_target_pairs={{1,0},{2,1},{3,2},{4,3},{5,4},{6,5},{7,6},{9,8},{10,9},{11,10},{12... | collective-permute-start | bytes 589832 | tf_op jit(solution)/shard_map/ppermute | solution.py:85
  443.0 7.0 %collective-permute-start.10 = (bf16[128,768]{1,0:T(8,128)(2,1)S(1)}, bf16[128,768]{1,0:T(8,128)(2,1)S(1)}, u32[]{:S(2)}, u32[]{:S(2)}) collective-permute-start(bf16[128,768]{1,0:T(8,128)(2,1)S(1)} %add_convert_fusion.12), channel_id=1, source_target_pairs={{1,0},{2,1},{3,2},{4,3},{5,4},{6,5},{7,6},{9,8},{10,9},{11,10},{12... | collective-permute-start | bytes 589832 | tf_op jit(solution)/shard_map/ppermute | solution.py:85
  453.6 7.0 %collective-permute-start.11 = (bf16[128,768]{1,0:T(8,128)(2,1)S(1)}, bf16[128,768]{1,0:T(8,128)(2,1)S(1)}, u32[]{:S(2)}, u32[]{:S(2)}) collective-permute-start(bf16[128,768]{1,0:T(8,128)(2,1)S(1)} %add_convert_fusion.11), channel_id=1, source_target_pairs={{1,0},{2,1},{3,2},{4,3},{5,4},{6,5},{7,6},{9,8},{10,9},{11,10},{12... | collective-permute-start | bytes 589832 | tf_op jit(solution)/shard_map/ppermute | solution.py:85
  455.8 89.4 %all-to-all-start.1 = ((bf16[128,4,768]{2,0,1:T(8,128)(2,1)}), bf16[128,4,768]{2,0,1:T(8,128)(2,1)S(1)}, u32[]{:S(2)}, u32[]{:S(2)}) async-start(bf16[128,4,768]{2,0,1:T(8,128)(2,1)} %bitcast.274), calls=%async_computation.3 | async-start | bytes 1572864 | tf_op jit(solution)/shard_map/all_to_all | solution.py:54
  459.4 135.0 %all-reduce.5.cloned.1.call-start = ((), (), s32[]{:S(2)}) async-start(), calls=%async_computation.7 | async-start | bytes 393216 | tf_op jit(solution)/shard_map/psum | solution.py:86
  469.7 15.4 %collective-permute-start.12 = (bf16[128,768]{1,0:T(8,128)(2,1)S(1)}, bf16[128,768]{1,0:T(8,128)(2,1)S(1)}, u32[]{:S(2)}, u32[]{:S(2)}) collective-permute-start(bf16[128,768]{1,0:T(8,128)(2,1)S(1)} %add_convert_fusion.10), channel_id=1, source_target_pairs={{1,0},{2,1},{3,2},{4,3},{5,4},{6,5},{7,6},{9,8},{10,9},{11,10},{12... | collective-permute-start | bytes 589832 | tf_op jit(solution)/shard_map/ppermute | solution.py:85
  491.1 28.6 %collective-permute-start.13 = (bf16[128,768]{1,0:T(8,128)(2,1)S(1)}, bf16[128,768]{1,0:T(8,128)(2,1)S(1)}, u32[]{:S(2)}, u32[]{:S(2)}) collective-permute-start(bf16[128,768]{1,0:T(8,128)(2,1)S(1)} %add_convert_fusion.9), channel_id=1, source_target_pairs={{1,0},{2,1},{3,2},{4,3},{5,4},{6,5},{7,6},{9,8},{10,9},{11,10},{12... | collective-permute-start | bytes 589832 | tf_op jit(solution)/shard_map/ppermute | solution.py:85
  545.3 94.4 %all-to-all-start = ((bf16[128,4,768]{2,0,1:T(8,128)(2,1)}), bf16[128,4,768]{2,0,1:T(8,128)(2,1)S(1)}, u32[]{:S(2)}, u32[]{:S(2)}) async-start(bf16[128,4,768]{2,0,1:T(8,128)(2,1)} %bitcast.275), calls=%async_computation.2 | async-start | bytes 1572864 | tf_op jit(solution)/shard_map/all_to_all | solution.py:54
  549.2 60.2 %copy-start.10 = (s32[512]{0:T(512)S(1)}, s32[512]{0:T(512)}, u32[]{:S(2)}) copy-start(s32[512]{0:T(512)} %get-tuple-element.13) | copy-start | bytes 6148
  609.4 30.3 %copy-start.1 = (bf16[512,768]{1,0:T(8,128)(2,1)S(1)}, bf16[512,768]{1,0:T(8,128)(2,1)}, u32[]{:S(2)}) copy-start(bf16[512,768]{1,0:T(8,128)(2,1)} %all_gather.29) | copy-start | bytes 2359300
  (18 other events, 157.0 us)
Sparse Core Ops, SparseCore 0:
  21.9 22.8 reduce-scatter.2
  46.3 49.6 all-gather.8
  97.5 50.3 all-gather.6
  236.9 60.3 all-reduce.2
  382.6 21.2 reduce-scatter.4
  531.3 63.0 all-reduce.4

commit v2 on v1

v2 whole, which is shorter than its diff:
```python
import functools

import jax
import jax.numpy as jnp
from jax import lax
from jax.experimental import pallas as pl
from jax.experimental.pallas import tpu as pltpu
from jax.sharding import PartitionSpec as P

NORM_EPS = 1e-6
MESH_ID = pl.DeviceIdType.MESH
GELU_C = 0.7978845608028654
GELU_A = 0.044715
BF16 = jnp.bfloat16
F32 = jnp.float32


def dot_of(lhs, rhs, lhs_dim, rhs_dim):
    return lax.dot_general(lhs, rhs, (((lhs_dim,), (rhs_dim,)), ((), ())), preferred_element_type=F32)


def row_chunk(rows):
    return max(size for size in range(16, 129, 16) if rows % size == 0)


def gelu_pair(hid):
    sq = hid * hid
    tanh = jnp.tanh(GELU_C * (hid + GELU_A * (hid * sq)))
    cdf = 0.5 * (1.0 + tanh)
    slope = cdf + (0.5 * GELU_C) * hid * (1.0 - tanh * tanh) * (1.0 + (3.0 * GELU_A) * sq)
    return hid * cdf, slope


def step_kernel(num_tp, num_pp, tile, x0, lab, e_hbm, w1_hbm, w2_hbm,
                loss_o, dw1_o, dw2_o, g_o, n_o, dx_o,
                x0r, w1s, w2s, x_in, y_buf, a_own, slope, n_all, x_all, a_cols, dy_all, dh_cols, dh_own, dy_in, dx_all,
                logit, stat, dn_send, dn_recv, g_buf,
                w_send, w_recv, p_send, p_recv, tp_send, tp_recv, tree_send, loc):
    rank = lax.axis_index('tp')
    stage = lax.axis_index('pp')
    last = num_pp - 1
    is_first = stage == 0
    is_last = stage == last
    _, seq, dim = x_in.shape
    vocab = e_hbm.shape[0]
    chunk = row_chunk(vocab)
    right = lax.rem(rank + 1, num_tp)
    left = lax.rem(rank + num_tp - 1, num_tp)
    opp = lax.rem(rank + 2, num_tp)
    X0, N, XA, AC, DY, DH, DX, ST, DN = range(9)

    def push(src, dst, ssem, rsem, dev):
        return pltpu.make_async_remote_copy(src_ref=src, dst_ref=dst, send_sem=ssem, recv_sem=rsem, device_id=dev, device_id_type=MESH_ID)

    def swap(kind, src_of, dst, mode):
        for k in range(1, num_tp):
            peer = lax.rem(rank + k, num_tp)
            if mode == 'recv':
                push(dst.at[peer], dst.at[peer], tp_send.at[kind, k], tp_recv.at[kind, peer], {'tp': rank}).wait_recv()
            else:
                copy = push(src_of(peer), dst.at[rank], tp_send.at[kind, k], tp_recv.at[kind, rank], {'tp': peer})
                copy.start() if mode == 'start' else copy.wait_send()

    num_x = num_pp // 2
    chip, core = stage // 2, lax.rem(stage, 2)

    def tree(kind, tid, buf, root, mode):
        root_x, root_c = root // 2, root % 2
        on_core = core == root_c
        partner = (chip * 2 + 1 - root_c)
        plus = lax.rem(chip + 1, num_x) * 2 + root_c
        minus = lax.rem(chip + num_x - 1, num_x) * 2 + root_c
        at_root = jnp.logical_and(on_core, chip == root_x)
        at_next = jnp.logical_and(on_core, jnp.logical_or(chip == root_x, chip == (root_x + 1) % num_x))
        for i in range(num_tp):
            blk = lax.rem(rank + i, num_tp)

            def go(slot, dest):
                copy = push(buf.at[blk], buf.at[blk], tree_send.at[tid, slot, i], tp_recv.at[kind, blk], {'pp': dest})
                copy.start() if mode == 'start' else copy.wait_send()

            if mode == 'start':
                wait = push(buf.at[blk], buf.at[blk], tree_send.at[tid, 0, i], tp_recv.at[kind, blk], {'pp': stage})
                if i == 0:
                    pl.when(stage != root)(wait.wait_recv)
                else:
                    wait.wait_recv()

            @pl.when(at_root)
            def _():
                go(0, minus)

            @pl.when(at_next)
            def _():
                go(1, plus)

            @pl.when(on_core)
            def _():
                go(2, partner)

    barrier = pltpu.get_barrier_semaphore()
    for k in range(1, num_tp):
        pl.semaphore_signal(barrier, inc=1, device_id={'tp': lax.rem(rank + k, num_tp)}, device_id_type=MESH_ID)
    for k in range(1, num_pp):
        pl.semaphore_signal(barrier, inc=1, device_id={'pp': lax.rem(stage + k, num_pp)}, device_id_type=MESH_ID)
    pl.semaphore_wait(barrier, num_tp + num_pp - 2)

    @pl.when(is_first)
    def _():
        swap(X0, lambda peer: x0.at[peer], x0r, 'start')

    own1 = pltpu.make_async_copy(w1_hbm, w1s.at[rank], loc.at[0])
    own2 = pltpu.make_async_copy(w2_hbm, w2s.at[rank], loc.at[1])
    own1.start()
    own2.start()

    def w_copy(idx):
        src, full, who, dev = [
            (w1_hbm, w1s, rank, right), (w2_hbm, w2s, rank, right), (w1_hbm, w1s, rank, left), (w2_hbm, w2s, rank, left),
            (w1s.at[left], w1s, left, right), (w2s.at[right], w2s, right, left)][idx]
        return push(src, full.at[who], w_send.at[idx], w_recv.at[idx], {'tp': dev})

    def w_wait(idx):
        full, who = [(w1s, left), (w2s, left), (w1s, right), (w2s, right), (w1s, opp), (w2s, opp)][idx]
        push(full.at[who], full.at[who], w_send.at[idx], w_recv.at[idx], {'tp': rank}).wait_recv()

    for idx in (0, 3, 1, 2):
        w_copy(idx).start()
    w_wait(0)
    w_copy(4).start()
    w_wait(3)
    w_copy(5).start()

    @pl.when(is_first)
    def _():
        swap(X0, None, x0r, 'recv')
        total = x0[rank].astype(F32)
        for k in range(1, num_tp):
            total = total + x0r[lax.rem(rank + k, num_tp)].astype(F32)
        x_in[0] = total.astype(BF16)

    for idx in (1, 2, 4, 5):
        w_wait(idx)
    own1.wait()
    own2.wait()

    fwd = push(y_buf.at[0], x_in.at[0], p_send.at[0], p_recv.at[0], {'pp': jnp.minimum(stage + 1, last)})
    bwd = push(y_buf.at[1], dy_in.at[0], p_send.at[1], p_recv.at[1], {'pp': jnp.maximum(stage - 1, 0)})

    @pl.when(jnp.logical_not(is_first))
    def _():
        fwd.wait_recv()

    x_act = x_in[0]
    total = x_act.astype(F32)
    for blk in range(num_tp):
        gate, grad = gelu_pair(dot_of(x_act, w1s[blk], 1, 0))
        a_own[blk] = gate.astype(BF16)
        slope[blk] = grad
        total = total + dot_of(a_own[blk], w2s[blk], 1, 0)
    y_buf[0] = total.astype(BF16)

    @pl.when(jnp.logical_not(is_last))
    def _():
        fwd.start()

    def norm_of():
        wide = y_buf[0].astype(F32)
        inv_rms = lax.rsqrt(jnp.mean(wide * wide, axis=-1, keepdims=True) + NORM_EPS)
        return inv_rms, wide * inv_rms

    @pl.when(is_last)
    def _():
        n_all[rank] = norm_of()[1].astype(BF16)
        swap(N, lambda peer: n_all.at[rank], n_all, 'start')

    tree(N, 0, n_all, last, 'start')
    x_all[rank] = x_in[0]
    a_cols[rank] = a_own[rank]
    swap(XA, lambda peer: x_in.at[0], x_all, 'start')
    swap(AC, lambda peer: a_own.at[peer], a_cols, 'start')
    n_out = pltpu.make_async_copy(n_all, n_o, loc.at[0])
    n_out.start()

    num_tok = num_tp * seq
    normed = n_all[...].reshape(num_tok, dim)
    full_tiles, tail = vocab // tile, vocab % tile
    lab_row = lab[...]
    rows_in = lax.broadcasted_iota(jnp.int32, (chunk // 8, 8, num_tok), 0) * 8 + lax.broadcasted_iota(jnp.int32, (chunk // 8, 8, num_tok), 1)

    def stats_of(base, count, carry):
        def one(c, carry):
            top, acc, hit = carry
            row = pl.multiple_of(base + c * chunk, chunk)
            part = logit[pl.ds(row, chunk), :].reshape(chunk // 8, 8, num_tok)
            new = jnp.maximum(top, jnp.max(part, axis=0))
            acc = acc * jnp.exp(top - new) + jnp.sum(jnp.exp(part - new[None]), axis=0)
            hit = hit + jnp.sum(jnp.where(rows_in == (lab_row - row)[None], part, 0.0), axis=0)
            return new, acc, hit
        return lax.fori_loop(0, count // chunk, one, carry)

    def logits_pass(e_buf):
        def fetch(i, size, slot):
            return pltpu.make_async_copy(e_hbm.at[pl.ds(pl.multiple_of(i * tile, 16), size)], e_buf.at[slot, pl.ds(0, size)], loc.at[2 + slot])

        def one(i, carry):
            slot = lax.rem(i, 2)

            @pl.when(i + 1 < full_tiles)
            def _():
                fetch(i + 1, tile, 1 - slot).start()
            fetch(i, tile, slot).wait()
            base = pl.multiple_of(i * tile, 16)
            logit[pl.ds(base, tile), :] = dot_of(e_buf[slot], normed, 1, 1)
            return stats_of(base, tile, carry)

        zero = jnp.zeros((8, num_tok), F32)
        fetch(0, tile, 0).start()
        carry = lax.fori_loop(0, full_tiles, one, (jnp.full((8, num_tok), -jnp.inf, F32), zero, zero))
        if tail:
            base = full_tiles * tile
            last_e = pltpu.make_async_copy(e_hbm.at[pl.ds(base, tail)], e_buf.at[0, pl.ds(0, tail)], loc.at[2])
            last_e.start()
            last_e.wait()
            logit[pl.ds(base, tail), :] = dot_of(e_buf[0, pl.ds(0, tail), :], normed, 1, 1)
            carry = stats_of(base, tail, carry)
        top, acc, hit = carry
        peak = jnp.max(top, axis=0, keepdims=True)
        total = jnp.sum(acc * jnp.exp(top - peak), axis=0, keepdims=True)
        hits = jnp.sum(hit, axis=0, keepdims=True)
        line = lax.broadcasted_iota(jnp.int32, (8, num_tok), 0)
        stat[rank] = jnp.where(line == 0, peak, jnp.where(line == 1, total, hits))

    pl.run_scoped(logits_pass, pltpu.VMEM((2, tile, dim), BF16))

    swap(ST, lambda peer: stat.at[rank], stat, 'start')
    swap(ST, None, stat, 'recv')
    peak = stat[0, 0:1, :]
    for j in range(1, num_tp):
        peak = jnp.maximum(peak, stat[j, 0:1, :])
    total = jnp.zeros_like(peak)
    target = jnp.zeros_like(peak)
    for j in range(num_tp):
        total = total + stat[j, 1:2, :] * jnp.exp(stat[j, 0:1, :] - peak)
        target = target + stat[j, 2:3, :]
    log_norm = peak + jnp.log(total)
    loss = jnp.sum(log_norm - target, axis=1, keepdims=True) / num_tok
    loss_o[...] = jnp.broadcast_to(loss, loss_o.shape)
    norm_rows = jnp.broadcast_to(log_norm, (8, num_tok))

    def grad_tile(base, count, slot):
        def one(c, carry):
            row = pl.multiple_of(base + c * chunk, chunk)
            part = logit[pl.ds(row, chunk), :].reshape(chunk // 8, 8, num_tok)
            hit = jnp.where(rows_in == (lab_row - row)[None], 1.0, 0.0)
            part = jnp.exp(part - norm_rows[None]) - hit
            g_buf[slot, pl.ds(pl.multiple_of(c * chunk, chunk), chunk), :] = part.reshape(chunk, num_tok).astype(BF16)
            return carry
        lax.fori_loop(0, count // chunk, one, 0)

    def grads_pass(e_buf, dn_acc):
        def fetch(base, size, slot):
            return pltpu.make_async_copy(e_hbm.at[pl.ds(base, size)], e_buf.at[slot, pl.ds(0, size)], loc.at[2 + slot])

        def put(base, size, slot):
            return pltpu.make_async_copy(g_buf.at[slot, pl.ds(0, size)], g_o.at[pl.ds(base, size)], loc.at[4 + slot])

        def at(i):
            return pl.multiple_of(i * tile, 16)

        @pl.when(is_last)
        def _():
            dn_acc[...] = jnp.zeros_like(dn_acc)
            fetch(0, tile, 0).start()

        def one(i, carry):
            slot = lax.rem(i, 2)

            @pl.when(i >= 2)
            def _():
                put(at(i - 2), tile, slot).wait()
            grad_tile(at(i), tile, slot)
            put(at(i), tile, slot).start()

            @pl.when(is_last)
            def _():
                @pl.when(i + 1 < full_tiles)
                def _():
                    fetch(at(i + 1), tile, 1 - slot).start()
                fetch(at(i), tile, slot).wait()
                dn_acc[...] += dot_of(g_buf[slot], e_buf[slot], 0, 0)
            return carry

        lax.fori_loop(0, full_tiles, one, 0)
        for i in range(max(full_tiles - 2, 0), full_tiles):
            put(i * tile, tile, i % 2).wait()
        if tail:
            base = full_tiles * tile

            @pl.when(is_last)
            def _():
                fetch(base, tail, 0).start()
            grad_tile(base, tail, 0)
            put(base, tail, 0).start()

            @pl.when(is_last)
            def _():
                fetch(base, tail, 0).wait()
                dn_acc[...] += dot_of(g_buf[0, pl.ds(0, tail), :], e_buf[0, pl.ds(0, tail), :], 0, 0)
            put(base, tail, 0).wait()

        @pl.when(is_last)
        def _():
            for k in range(num_tp):
                dn_send[k] = dn_acc[k * seq:(k + 1) * seq, :].astype(BF16)
            swap(DN, lambda peer: dn_send.at[peer], dn_recv, 'start')
            swap(DN, None, dn_recv, 'recv')
            grad_n = dn_acc[pl.ds(pl.multiple_of(rank * seq, seq), seq), :]
            for k in range(1, num_tp):
                grad_n = grad_n + dn_recv[lax.rem(rank + k, num_tp)].astype(F32)
            inv_rms, unit = norm_of()
            dy_in[0] = (inv_rms * (grad_n - unit * jnp.mean(unit * grad_n, axis=-1, keepdims=True))).astype(BF16)

    pl.run_scoped(grads_pass, pltpu.VMEM((2, tile, dim), BF16), pltpu.VMEM((num_tok, dim), F32))

    @pl.when(jnp.logical_not(is_last))
    def _():
        bwd.wait_recv()

    grad_y = dy_in[0]
    total = grad_y.astype(F32)
    for blk in range(num_tp):
        grad_h = (slope[blk] * dot_of(grad_y, w2s[blk], 1, 1)).astype(BF16)
        dh_own[blk] = grad_h
        total = total + dot_of(grad_h, w1s[blk], 1, 1)
    y_buf[1] = total.astype(BF16)

    @pl.when(jnp.logical_not(is_first))
    def _():
        bwd.start()

    @pl.when(is_first)
    def _():
        dx_all[rank] = y_buf[1]
        swap(DX, lambda peer: y_buf.at[1], dx_all, 'start')
        tree(DX, 1, dx_all, 0, 'start')

    dy_all[rank] = dy_in[0]
    dh_cols[rank] = dh_own[rank]
    swap(DY, lambda peer: dy_in.at[0], dy_all, 'start')
    swap(DH, lambda peer: dh_own.at[peer], dh_cols, 'start')
    for kind, dst in ((XA, x_all), (AC, a_cols), (DY, dy_all), (DH, dh_cols)):
        swap(kind, None, dst, 'recv')

    def weight_grads(dw):
        dw[0] = dot_of(a_cols[...].reshape(num_tok, a_cols.shape[2]), dy_all[...].reshape(num_tok, dim), 0, 0)
        out2 = pltpu.make_async_copy(dw.at[0], dw2_o, loc.at[2])
        out2.start()
        dw[1] = dot_of(x_all[...].reshape(num_tok, dim), dh_cols[...].reshape(num_tok, dh_cols.shape[2]), 0, 0)
        out1 = pltpu.make_async_copy(dw.at[1], dw1_o, loc.at[3])
        out1.start()
        out2.wait()
        out1.wait()

    pl.run_scoped(weight_grads, pltpu.VMEM((2, dim, dim), F32))

    @pl.when(jnp.logical_not(is_first))
    def _():
        tree(DX, 1, dx_all, 0, 'start')
    dx_out = pltpu.make_async_copy(dx_all, dx_o, loc.at[1])
    dx_out.start()

    for idx in range(6):
        w_copy(idx).wait_send()

    @pl.when(is_first)
    def _():
        swap(X0, lambda peer: x0.at[peer], x0r, 'sent')
        swap(DX, lambda peer: y_buf.at[1], dx_all, 'sent')

    @pl.when(is_last)
    def _():
        swap(N, lambda peer: n_all.at[rank], n_all, 'sent')
        swap(DN, lambda peer: dn_send.at[peer], dn_recv, 'sent')

    @pl.when(jnp.logical_not(is_last))
    def _():
        fwd.wait_send()

    @pl.when(jnp.logical_not(is_first))
    def _():
        bwd.wait_send()
    swap(XA, lambda peer: x_in.at[0], x_all, 'sent')
    swap(AC, lambda peer: a_own.at[peer], a_cols, 'sent')
    swap(ST, lambda peer: stat.at[rank], stat, 'sent')
    swap(DY, lambda peer: dy_in.at[0], dy_all, 'sent')
    swap(DH, lambda peer: dh_own.at[peer], dh_cols, 'sent')
    tree(N, 0, n_all, last, 'sent')
    tree(DX, 1, dx_all, 0, 'sent')
    n_out.wait()
    dx_out.wait()


def table_kernel(block, tok, n_all, dx_all, g_ref, out_ref):
    num_tok = tok.shape[1]
    rows = lax.broadcasted_iota(jnp.int32, (block, num_tok), 0) + pl.program_id(0) * block
    one_hot = jnp.where(rows == tok[...], 1.0, 0.0).astype(BF16)
    out_ref[...] = dot_of(g_ref[...], n_all[...], 1, 0) + dot_of(one_hot, dx_all[...], 1, 0)


def solution(mesh):
    num_tp, num_pp = mesh.shape['tp'], mesh.shape['pp']

    def device_fn(tokens, labels, emb_table, w_in, w_out):
        num_micro, seq = tokens.shape
        vocab, dim = emb_table.shape
        cols = w_in.shape[2]
        num_tok = num_micro * seq
        base = lax.axis_index('tp') * vocab
        tok_local = tokens - base
        owned = (tok_local >= 0) & (tok_local < vocab)
        looked_up = jnp.take(emb_table, jnp.clip(tok_local, 0, vocab - 1), axis=0)
        x0 = jnp.where(owned[:, :, None], looked_up, jnp.zeros_like(looked_up))
        lab_row = (labels - base).reshape(1, num_tok)
        tok_row = tok_local.reshape(1, num_tok)
        chunk = row_chunk(vocab)
        tile = chunk * min(10, max(1, vocab // chunk // 3))
        vmem, hbm = pl.BlockSpec(memory_space=pltpu.VMEM), pl.BlockSpec(memory_space=pl.ANY)
        act = (num_tp, seq, dim)
        wide = (num_tp, seq, cols)
        shape = jax.ShapeDtypeStruct
        dma = pltpu.SemaphoreType.DMA
        loss, grad_one, grad_two, g_all, n_all, dx_all = pl.pallas_call(
            functools.partial(step_kernel, num_tp, num_pp, tile),
            out_shape=(shape((8, 128), F32), shape((dim, cols), F32), shape((cols, dim), F32), shape((vocab, num_tok), BF16),
                       shape(act, BF16), shape(act, BF16)),
            in_specs=[vmem, vmem, hbm, hbm, hbm],
            out_specs=(vmem, hbm, hbm, hbm, hbm, hbm),
            scratch_shapes=[
                pltpu.VMEM(act, BF16), pltpu.VMEM((num_tp, dim, cols), BF16), pltpu.VMEM((num_tp, cols, dim), BF16),
                pltpu.VMEM((1, seq, dim), BF16), pltpu.VMEM((2, seq, dim), BF16), pltpu.VMEM(wide, BF16), pltpu.VMEM(wide, F32),
                pltpu.VMEM(act, BF16), pltpu.VMEM(act, BF16), pltpu.VMEM(wide, BF16), pltpu.VMEM(act, BF16), pltpu.VMEM(wide, BF16),
                pltpu.VMEM(wide, BF16), pltpu.VMEM((1, seq, dim), BF16), pltpu.VMEM(act, BF16),
                pltpu.VMEM((vocab, num_tok), F32), pltpu.VMEM((num_tp, 8, num_tok), F32), pltpu.VMEM(act, BF16), pltpu.VMEM(act, BF16),
                pltpu.VMEM((2, tile, num_tok), BF16),
                dma((6,)), dma((6,)), dma((2,)), dma((2,)), dma((9, num_tp)), dma((9, num_tp)), dma((2, 3, num_tp)), dma((6,)),
            ],
            compiler_params=pltpu.CompilerParams(collective_id=0, has_side_effects=True, vmem_limit_bytes=67043328),
            name='step_kernel',
        )(x0, lab_row, emb_table, w_in[0], w_out[0])

        block = chunk * min(10, max(1, vocab // chunk // 3))
        whole = lambda shp: pl.BlockSpec(shp, lambda i: (0, 0))
        grad_table = pl.pallas_call(
            functools.partial(table_kernel, block),
            grid=(pl.cdiv(vocab, block),),
            out_shape=shape((vocab, dim), F32),
            in_specs=[whole((1, num_tok)), whole((num_tok, dim)), whole((num_tok, dim)), pl.BlockSpec((block, num_tok), lambda i: (i, 0))],
            out_specs=pl.BlockSpec((block, dim), lambda i: (i, 0)),
            compiler_params=pltpu.CompilerParams(dimension_semantics=('arbitrary',), vmem_limit_bytes=48 * 1024 * 1024),
            name='table_kernel',
        )(tok_row, n_all.reshape(num_tok, dim), dx_all.reshape(num_tok, dim), g_all)
        return loss[0, :1], grad_one[None], grad_two[None], grad_table

    return jax.shard_map(device_fn, mesh=mesh, in_specs=(P('dp', None), P('dp', None), P('tp', None), P('pp', None, 'tp'), P('pp', 'tp', None)), out_specs=(P('dp'), P(('dp', 'pp'), None, 'tp'), P(('dp', 'pp'), 'tp', None), P(('dp', 'tp'), None)), check_vma=False)
```

time: 659 us -> 315 us (0.48); the launches traced: 650 us -> 314 us
  Pallas kernels: 0 us -> 290 us
  waiting for transfers between devices: 272 us -> 0 us
  matrix products: 203 us -> 0 us
  blocking collectives: 70.2 us -> 0 us
  starting transfers between devices: 54.6 us -> 0 us
  other arithmetic: 20.1 us -> 3.06 us
  between operations: 17 us -> 0.66 us
    pallas_call x0 -> x2, Pallas kernels: none -> 290 us  [the longest x1 263 us: device_fn(): pl.pallas_call(functools.partial(step_kernel, num_tp, num_pp, tile), out_...]
    dot_general x31 -> x0, matrix products: 203 us -> none  [the longest x22 153 us: contract(): lax.dot_general(lhs, rhs, (((lhs_dim,), (rhs_dim,)), ((), ())), preferred...]
    psum x2 -> x0, waiting for transfers between devices: 103 us -> none  [the longest x1 60.5 us: device_fn(): y_top = lax.psum(jnp.where(is_last, y_act, jnp.zeros_like(y_act)), 'pp')]
    all_gather x2 -> x0, waiting for transfers between devices: 103 us -> none  [the longest x1 52 us: device_fn(): w_one = lax.all_gather(w_in[0], 'tp', axis=1, tiled=True)]
    all_gather x5 -> x0, blocking collectives: 70.2 us -> none  [the longest x1 15 us: device_fn(): lax.all_gather(lax.psum(jnp.where(is_first, grad_x, jnp.zeros_like(grad_x...]
    ppermute x14 -> x0, starting transfers between devices: 46.5 us -> none  [the longest x7 37.1 us: device_fn(): x_act = lax.ppermute(y_act, 'pp', fwd_perm)]
    reduce_scatter x2 -> x0, waiting for transfers between devices: 37.1 us -> none  [the longest x1 21.3 us: device_fn(): lax.psum_scatter(jnp.where(owned_ids[:, :, None], looked_up, jnp.zeros_li...]
    ppermute x14 -> x0, waiting for transfers between devices: 26.3 us -> none  [the longest x7 19.3 us: device_fn(): grad_y = lax.ppermute(grad_x, 'pp', bwd_perm)]
  transfers between devices with their start and end apart: 22 -> 0, of which waited for: 18 -> 0; matrix products, arithmetic and copies ran while one was open for 14% -> 0% of each run, Pallas kernels for 0% -> 0%
where the time goes in v2:
time: 315 us; the launch traced here: 314 us
  Pallas kernels  290 us (92%)
  local copies, waits for them, and re-layouts  20 us (6%)
    pallas_call x1, Pallas kernels, device_fn(): pl.pallas_call(functools.partial(step_kernel, num_tp, num_pp, tile), out_...  263 us
    pallas_call x1, Pallas kernels, device_fn(): pl.pallas_call(functools.partial(table_kernel, block), grid=(pl.cdiv(voca...  27.5 us
    gather x1, local copies, waits for them, and re-layouts, device_fn(): looked_up = jnp.take(emb_table, jnp.clip(tok_local, 0, vocab - 1), axis=0)  11.4 us
    unnamed x14, local copies, waits for them, and re-layouts  7.44 us

profile of v2, /device:TPU:96, one launch (start us, length us, event | category | flops | bytes accessed | tf_op | source)
XLA Modules:
  0.0 313.8 jit_solution(3653693530705242861)
XLA Ops:
  0.6 1.3 broadcast_subtract_fusion
  1.9 0.7 compare_and_fusion.1
  2.6 0.0 copy-start.2
  2.6 0.6 copy-done.2
  3.2 11.4 %gather_fusion = bf16[512,768]{1,0:T(8,128)(2,1)S(1)} fusion(bf16[12576,768]{1,0:T(8,128)(2,1)} %e_hbm.1, s32[1024]{0:T(1024)S(1)} %pad_clamp_fusion), kind=kCustom, calls=%fused_computation | custom fusion | bytes 1574912 | tf_op jit(solution)/shard_map/jit(_take)/gather | solution.py:422
  14.6 1.1 select_select_fusion.x0
  15.6 262.7 %step_kernel.1 = (f32[8,128]{1,0:T(8,128)}, f32[768,768]{1,0:T(8,128)}, f32[768,768]{1,0:T(8,128)}, bf16[12576,512]{1,0:T(8,128)(2,1)}, bf16[4,128,768]{2,1,0:T(8,128)(2,1)}, /*index=5*/bf16[4,128,768]{2,1,0:T(8,128)(2,1)}) custom-call(bf16[4,128,768]{2,1,0:T(8,128)(2,1)} %select_select_fusion.x0, s32[1,512]{1,0:T(1,128)} %bitcast.20, ...), custom_call_target="tpu_custom_call" | custom-call | tf_op jit(solution)/shard_map/step_kernel/pallas_call | solution.py:433
  278.3 1.2 slice.3
  279.5 0.0 copy-start
  279.5 1.1 copy-done
  280.6 0.0 copy-start.1
  280.6 1.1 copy-done.1
  281.8 0.0 copy-start.3
  281.8 0.7 copy-done.3
  282.5 0.0 copy-start.5
  282.5 27.5 %table_kernel.1 = f32[12576,768]{1,0:T(8,128)} custom-call(s32[1,512]{1,0:T(1,128)S(1)} %bitcast.14, bf16[512,768]{1,0:T(8,128)(2,1)S(1)} %bitcast.12, bf16[512,768]{1,0:T(8,128)(2,1)S(1)} %bitcast.13, bf16[12576,512]{1,0:T(8,128)(2,1)} %get-tuple-element.15.g_ref), custom_call_target="tpu_custom_call" | custom-call | tf_op jit(solution)/shard_map/table_kernel/pallas_call | solution.py:454
  309.9 0.0 copy-done.5
  309.9 0.0 copy-start.4
  309.9 1.4 copy.11
  311.3 1.1 copy-done.4
  312.4 1.4 copy.12
  (3 shorter events, 0.0 us)
Async XLA Ops:
  2.6 0.6 copy-start.2
  279.5 1.1 copy-start
  280.6 1.1 copy-start.1
  281.8 0.7 copy-start.3
  282.5 27.5 %copy-start.5 = (f32[768,768]{1,0:T(8,128)S(1)}, f32[768,768]{1,0:T(8,128)}, u32[]{:S(2)}) copy-start(f32[768,768]{1,0:T(8,128)} %get-tuple-element.11) | copy-start | bytes 7077892
  309.9 2.5 copy-start.4

commit v3 on v2

v3 whole, which is shorter than its diff:
```python
import functools

import jax
import jax.numpy as jnp
from jax import lax
from jax.experimental import pallas as pl
from jax.experimental.pallas import tpu as pltpu
from jax.sharding import PartitionSpec as P

NORM_EPS = 1e-6
MESH_ID = pl.DeviceIdType.MESH
GELU_C = 0.7978845608028654
GELU_A = 0.044715
BF16 = jnp.bfloat16
F32 = jnp.float32


def dot_of(lhs, rhs, lhs_dim, rhs_dim):
    return lax.dot_general(lhs, rhs, (((lhs_dim,), (rhs_dim,)), ((), ())), preferred_element_type=F32)


def row_chunk(rows):
    return max(size for size in range(16, 129, 16) if rows % size == 0)


def gelu_pair(hid):
    sq = hid * hid
    tanh = jnp.tanh(GELU_C * (hid + GELU_A * (hid * sq)))
    cdf = 0.5 * (1.0 + tanh)
    slope = cdf + (0.5 * GELU_C) * hid * (1.0 - tanh * tanh) * (1.0 + (3.0 * GELU_A) * sq)
    return hid * cdf, slope


def step_kernel(num_tp, num_pp, tile, half, tok, lab, e_hbm, w1_hbm, w2_hbm,
                loss_o, meta_o, g_o, n_o, dx_o, xa_o, ac_o, dy_o, dh_o,
                x0, x0r, w1s, w2s, x_in, y_buf, a_own, slope, n_all, x_all, a_cols, dy_all, dh_cols, dh_own, dy_in, dx_all,
                logit, stat, dn_send, dn_recv, dn_half, g_buf, key_buf,
                w_send, w_recv, p_send, p_recv, tp_send, tp_recv, tree_send, st_send, st_recv, g_send, g_recv, out_sem, loc):
    rank = lax.axis_index('tp')
    stage = lax.axis_index('pp')
    last = num_pp - 1
    is_first = stage == 0
    is_last = stage == last
    _, seq, dim = x_in.shape
    vocab = e_hbm.shape[0]
    chunk = row_chunk(vocab)
    right = lax.rem(rank + 1, num_tp)
    left = lax.rem(rank + num_tp - 1, num_tp)
    opp = lax.rem(rank + 2, num_tp)
    X0, N, XA, AC, DY, DH, DX, DN = range(8)

    def push(src, dst, ssem, rsem, dev):
        return pltpu.make_async_remote_copy(src_ref=src, dst_ref=dst, send_sem=ssem, recv_sem=rsem, device_id=dev, device_id_type=MESH_ID)

    def swap(kind, src_of, dst, mode):
        for k in range(1, num_tp):
            peer = lax.rem(rank + k, num_tp)
            if mode == 'recv':
                push(dst.at[peer], dst.at[peer], tp_send.at[kind, k], tp_recv.at[kind, peer], {'tp': rank}).wait_recv()
            else:
                copy = push(src_of(peer), dst.at[rank], tp_send.at[kind, k], tp_recv.at[kind, rank], {'tp': peer})
                copy.start() if mode == 'start' else copy.wait_send()

    num_x = num_pp // 2
    chip, core = stage // 2, lax.rem(stage, 2)
    partner = chip * 2 + 1 - core
    is_top = chip == num_x - 1

    def tree(kind, tid, buf, root, mode):
        root_x, root_c = root // 2, root % 2
        on_core = core == root_c
        plus = lax.rem(chip + 1, num_x) * 2 + root_c
        minus = lax.rem(chip + num_x - 1, num_x) * 2 + root_c
        at_root = jnp.logical_and(on_core, chip == root_x)
        at_next = jnp.logical_and(on_core, jnp.logical_or(chip == root_x, chip == (root_x + 1) % num_x))
        for i in range(num_tp):
            blk = lax.rem(rank + i, num_tp)

            def go(slot, dest):
                copy = push(buf.at[blk], buf.at[blk], tree_send.at[tid, slot, i], tp_recv.at[kind, blk], {'pp': dest})
                copy.start() if mode == 'start' else copy.wait_send()

            if mode == 'start':
                wait = push(buf.at[blk], buf.at[blk], tree_send.at[tid, 0, i], tp_recv.at[kind, blk], {'pp': stage})
                if i == 0:
                    pl.when(stage != root)(wait.wait_recv)
                else:
                    wait.wait_recv()

            @pl.when(on_core)
            def _():
                go(2, partner)

            @pl.when(at_root)
            def _():
                go(0, minus)

            @pl.when(at_next)
            def _():
                go(1, plus)

    barrier = pltpu.get_barrier_semaphore()
    for k in range(1, num_tp):
        for pp in (stage, partner):
            pl.semaphore_signal(barrier, inc=1, device_id={'tp': lax.rem(rank + k, num_tp), 'pp': pp}, device_id_type=MESH_ID)
    for k in range(1, num_pp):
        pl.semaphore_signal(barrier, inc=1, device_id={'pp': lax.rem(stage + k, num_pp)}, device_id_type=MESH_ID)
    pl.semaphore_wait(barrier, 2 * (num_tp - 1) + num_pp - 1)

    own1 = pltpu.make_async_copy(w1_hbm, w1s.at[rank], loc.at[0])
    own2 = pltpu.make_async_copy(w2_hbm, w2s.at[rank], loc.at[1])
    own1.start()
    own2.start()

    def w_copy(idx):
        src, full, who, dev = [
            (w1_hbm, w1s, rank, right), (w2_hbm, w2s, rank, right), (w1_hbm, w1s, rank, left), (w2_hbm, w2s, rank, left),
            (w1s.at[left], w1s, left, right), (w2s.at[right], w2s, right, left)][idx]
        return push(src, full.at[who], w_send.at[idx], w_recv.at[idx], {'tp': dev})

    def w_wait(idx):
        full, who = [(w1s, left), (w2s, left), (w1s, right), (w2s, right), (w1s, opp), (w2s, opp)][idx]
        push(full.at[who], full.at[who], w_send.at[idx], w_recv.at[idx], {'tp': rank}).wait_recv()

    for idx in (0, 3, 1, 2):
        w_copy(idx).start()

    num_tok = num_tp * seq
    vocab_base = rank * vocab
    tail_base = (2 * half - 1) * tile
    tail = vocab - tail_base
    tok_row = tok[...] - vocab_base
    lab_row = lab[...] - vocab_base
    rows_in = lax.broadcasted_iota(jnp.int32, (chunk // 8, 8, num_tok), 0) * 8 + lax.broadcasted_iota(jnp.int32, (chunk // 8, 8, num_tok), 1)

    def at(i):
        return pl.multiple_of(i * tile, 16)

    def fetch(e_buf, base, size, slot):
        return pltpu.make_async_copy(e_hbm.at[pl.ds(base, size)], e_buf.at[slot, pl.ds(0, size)], loc.at[2 + slot])

    def sort_tokens():
        key_row = jnp.where(jnp.logical_and(tok_row >= 0, tok_row < vocab), tok_row, 1 << 20).astype(F32)
        lanes = lax.broadcasted_iota(jnp.int32, (1, num_tok), 1).astype(F32)
        step = 128
        key_buf[...] = jnp.transpose(jnp.broadcast_to(key_row, (step, num_tok)))

        def count(b, pos):
            here = key_buf[pl.ds(pl.multiple_of(b * step, step), step), 0:1]
            idx = (lax.broadcasted_iota(jnp.int32, (step, 1), 0) + b * step).astype(F32)
            ahead = jnp.logical_or(here < key_row, jnp.logical_and(here == key_row, idx < lanes))
            return pos + jnp.sum(jnp.where(ahead, 1.0, 0.0), axis=0, keepdims=True)

        def starts(b, acc):
            here = key_buf[pl.ds(pl.multiple_of(b * step, step), step), 0:1]
            return acc + jnp.sum(jnp.where(here < lanes * tile, 1.0, 0.0), axis=0, keepdims=True)

        zero = jnp.zeros((1, num_tok), F32)
        pos_row = lax.fori_loop(0, num_tok // step, count, zero)
        offs = lax.fori_loop(0, num_tok // step, starts, zero)

        def place(b, carry):
            keys, idxs = carry
            here = key_buf[pl.ds(pl.multiple_of(b * step, step), step), 0:1]
            pos = key_buf[pl.ds(pl.multiple_of(b * step, step), step), 1:2]
            idx = (lax.broadcasted_iota(jnp.int32, (step, 1), 0) + b * step).astype(F32)
            mine = pos == lanes
            keys = keys + jnp.sum(jnp.where(mine, here, 0.0), axis=0, keepdims=True)
            return keys, idxs + jnp.sum(jnp.where(mine, idx, 0.0), axis=0, keepdims=True)

        both = jnp.where(lax.broadcasted_iota(jnp.int32, (step, num_tok), 0) == 0, key_row, pos_row)
        key_buf[...] = jnp.transpose(both)
        keys, idxs = lax.fori_loop(0, num_tok // step, place, (zero, zero))
        line = lax.broadcasted_iota(jnp.int32, (8, num_tok), 0)
        meta_o[...] = jnp.where(line == 0, keys, jnp.where(line == 1, idxs, offs)).astype(jnp.int32)

    sort_tokens()

    def lookup_pass(e_buf, acc):
        def tile_of(base, size, slot):
            def one(c, carry):
                row = base + c * chunk
                hot = jnp.where(rows_in == (tok_row - row)[None], 1.0, 0.0)
                g_buf[slot, pl.ds(pl.multiple_of(c * chunk, chunk), chunk), :] = hot.reshape(chunk, num_tok).astype(BF16)
                return carry
            lax.fori_loop(0, size // chunk, one, 0)
            fetch(e_buf, base, size, slot).wait()
            acc[...] += dot_of(g_buf[slot, pl.ds(0, size), :], e_buf[slot, pl.ds(0, size), :], 0, 0)

        acc[...] = jnp.zeros_like(acc)
        fetch(e_buf, 0, tile, 0).start()
        count = 2 * half - 1

        def one(i, carry):
            slot = lax.rem(i, 2)

            @pl.when(i + 1 < count)
            def _():
                fetch(e_buf, at(i + 1), tile, 1 - slot).start()
            tile_of(at(i), tile, slot)
            return carry
        lax.fori_loop(0, count, one, 0)
        fetch(e_buf, tail_base, tail, 0).start()
        tile_of(tail_base, tail, 0)
        for k in range(num_tp):
            x0[k] = acc[k * seq:(k + 1) * seq, :].astype(BF16)

    @pl.when(is_first)
    def _():
        pl.run_scoped(lookup_pass, pltpu.VMEM((2, tile, dim), BF16), pltpu.VMEM((num_tok, dim), F32))
        swap(X0, lambda peer: x0.at[peer], x0r, 'start')

    w_wait(0)
    w_copy(4).start()
    w_wait(3)
    w_copy(5).start()

    @pl.when(is_first)
    def _():
        swap(X0, None, x0r, 'recv')
        total = x0[rank].astype(F32)
        for k in range(1, num_tp):
            total = total + x0r[lax.rem(rank + k, num_tp)].astype(F32)
        x_in[0] = total.astype(BF16)

    for idx in (1, 2, 4, 5):
        w_wait(idx)
    own1.wait()
    own2.wait()

    fwd = push(y_buf.at[0], x_in.at[0], p_send.at[0], p_recv.at[0], {'pp': jnp.minimum(stage + 1, last)})
    bwd = push(y_buf.at[1], dy_in.at[0], p_send.at[1], p_recv.at[1], {'pp': jnp.maximum(stage - 1, 0)})

    @pl.when(jnp.logical_not(is_first))
    def _():
        fwd.wait_recv()

    x_act = x_in[0]
    total = x_act.astype(F32)
    for blk in range(num_tp):
        gate, grad = gelu_pair(dot_of(x_act, w1s[blk], 1, 0))
        a_own[blk] = gate.astype(BF16)
        slope[blk] = grad
        total = total + dot_of(a_own[blk], w2s[blk], 1, 0)
    y_buf[0] = total.astype(BF16)

    @pl.when(jnp.logical_not(is_last))
    def _():
        fwd.start()

    def norm_of():
        wide = y_buf[0].astype(F32)
        inv_rms = lax.rsqrt(jnp.mean(wide * wide, axis=-1, keepdims=True) + NORM_EPS)
        return inv_rms, wide * inv_rms

    @pl.when(is_last)
    def _():
        n_all[rank] = norm_of()[1].astype(BF16)
        swap(N, lambda peer: n_all.at[rank], n_all, 'start')

    tree(N, 0, n_all, last, 'start')
    x_all[rank] = x_in[0]
    a_cols[rank] = a_own[rank]
    swap(XA, lambda peer: x_in.at[0], x_all, 'start')
    swap(AC, lambda peer: a_own.at[peer], a_cols, 'start')
    outs = [(n_all, n_o), (dx_all, dx_o), (x_all, xa_o), (a_cols, ac_o), (dy_all, dy_o), (dh_cols, dh_o)]

    def out_copy(idx):
        return pltpu.make_async_copy(outs[idx][0], outs[idx][1], out_sem.at[idx])

    out_copy(0).start()
    normed = n_all[...].reshape(num_tok, dim)
    base0 = core * (half * tile)
    mine = half - core
    is_odd = core == 1

    def stats_of(base, count, carry):
        def one(c, carry):
            top, acc, hit = carry
            row = pl.multiple_of(base + c * chunk, chunk)
            part = logit[pl.ds(row, chunk), :].reshape(chunk // 8, 8, num_tok)
            new = jnp.maximum(top, jnp.max(part, axis=0))
            acc = acc * jnp.exp(top - new) + jnp.sum(jnp.exp(part - new[None]), axis=0)
            hit = hit + jnp.sum(jnp.where(rows_in == (lab_row - (base0 + row))[None], part, 0.0), axis=0)
            return new, acc, hit
        return lax.fori_loop(0, count // chunk, one, carry)

    slot_of = rank * 2 + core

    def logits_pass(e_buf):
        def finish(carry):
            top, acc, hit = carry
            peak = jnp.max(top, axis=0, keepdims=True)
            total = jnp.sum(acc * jnp.exp(top - peak), axis=0, keepdims=True)
            hits = jnp.sum(hit, axis=0, keepdims=True)
            line = lax.broadcasted_iota(jnp.int32, (8, num_tok), 0)
            stat[slot_of] = jnp.where(line == 0, peak, jnp.where(line == 1, total, hits))

        def one(i, carry):
            slot = lax.rem(i, 2)

            @pl.when(i + 1 < mine)
            def _():
                fetch(e_buf, base0 + at(i + 1), tile, 1 - slot).start()
            fetch(e_buf, base0 + at(i), tile, slot).wait()
            logit[pl.ds(at(i), tile), :] = dot_of(e_buf[slot], normed, 1, 1)
            return stats_of(at(i), tile, carry)

        zero = jnp.zeros((8, num_tok), F32)
        fetch(e_buf, base0, tile, 0).start()
        carry = lax.fori_loop(0, mine, one, (jnp.full((8, num_tok), -jnp.inf, F32), zero, zero))

        @pl.when(is_odd)
        def _():
            slot = (half - 1) % 2
            fetch(e_buf, tail_base, tail, slot).start()
            fetch(e_buf, tail_base, tail, slot).wait()
            logit[pl.ds((half - 1) * tile, tail), :] = dot_of(e_buf[slot, pl.ds(0, tail), :], normed, 1, 1)
            finish(stats_of((half - 1) * tile, tail, carry))

        @pl.when(jnp.logical_not(is_odd))
        def _():
            finish(carry)

    pl.run_scoped(logits_pass, pltpu.VMEM((2, tile, dim), BF16))

    def stats_swap(mode):
        for k in range(num_tp):
            for flip in range(2):
                if k == 0 and flip == 0:
                    continue
                peer = lax.rem(rank + k, num_tp)
                peer_core = core if flip == 0 else 1 - core
                theirs = peer * 2 + peer_core
                if mode == 'recv':
                    push(stat.at[theirs], stat.at[theirs], st_send.at[2 * k + flip], st_recv.at[theirs], {'tp': rank}).wait_recv()
                else:
                    copy = push(stat.at[slot_of], stat.at[slot_of], st_send.at[2 * k + flip], st_recv.at[slot_of],
                                {'tp': peer, 'pp': chip * 2 + peer_core})
                    copy.start() if mode == 'start' else copy.wait_send()

    stats_swap('start')
    stats_swap('recv')
    peak = stat[0, 0:1, :]
    for j in range(1, 2 * num_tp):
        peak = jnp.maximum(peak, stat[j, 0:1, :])
    total = jnp.zeros_like(peak)
    target = jnp.zeros_like(peak)
    for j in range(2 * num_tp):
        total = total + stat[j, 1:2, :] * jnp.exp(stat[j, 0:1, :] - peak)
        target = target + stat[j, 2:3, :]
    log_norm = peak + jnp.log(total)
    loss = jnp.sum(log_norm - target, axis=1, keepdims=True) / num_tok
    loss_o[...] = jnp.broadcast_to(loss, loss_o.shape)
    norm_rows = jnp.broadcast_to(log_norm, (8, num_tok))

    def grad_tile(base, count, slot):
        def one(c, carry):
            row = pl.multiple_of(base + c * chunk, chunk)
            part = logit[pl.ds(row, chunk), :].reshape(chunk // 8, 8, num_tok)
            hit = jnp.where(rows_in == (lab_row - (base0 + row))[None], 1.0, 0.0)
            part = jnp.exp(part - norm_rows[None]) - hit
            g_buf[slot, pl.ds(pl.multiple_of(c * chunk, chunk), chunk), :] = part.reshape(chunk, num_tok).astype(BF16)
            return carry
        lax.fori_loop(0, count // chunk, one, 0)

    def g_copies(i, base, size, slot):
        here, there = g_buf.at[slot, pl.ds(0, size)], g_o.at[pl.ds(base, size)]
        return pltpu.make_async_copy(here, there, loc.at[4 + slot]), push(here, there, g_send.at[slot], g_recv.at[i], {'pp': partner})

    def g_start(i, base, size, slot):
        for copy in g_copies(i, base, size, slot):
            copy.start()

    def g_wait(i, base, size, slot):
        keep, send = g_copies(i, base, size, slot)
        keep.wait()
        send.wait_send()

    def grads_pass(e_buf, dn_acc):
        @pl.when(is_top)
        def _():
            dn_acc[...] = jnp.zeros_like(dn_acc)
            fetch(e_buf, base0, tile, 0).start()

        def one(i, carry):
            slot = lax.rem(i, 2)

            @pl.when(i >= 2)
            def _():
                g_wait(i - 2, base0 + at(i - 2), tile, slot)
            grad_tile(at(i), tile, slot)
            g_start(i, base0 + at(i), tile, slot)

            @pl.when(is_top)
            def _():
                @pl.when(i + 1 < mine)
                def _():
                    fetch(e_buf, base0 + at(i + 1), tile, 1 - slot).start()
                fetch(e_buf, base0 + at(i), tile, slot).wait()
                dn_acc[...] += dot_of(g_buf[slot], e_buf[slot], 0, 0)
            return carry

        lax.fori_loop(0, mine, one, 0)
        final = half - 1
        slot = final % 2

        @pl.when(is_odd)
        def _():
            @pl.when(is_top)
            def _():
                fetch(e_buf, tail_base, tail, slot).start()
            if final >= 2:
                g_wait(final - 2, base0 + (final - 2) * tile, tile, slot)
            grad_tile(final * tile, tail, slot)
            g_start(final, tail_base, tail, slot)

            @pl.when(is_top)
            def _():
                fetch(e_buf, tail_base, tail, slot).wait()
                dn_acc[...] += dot_of(g_buf[slot, pl.ds(0, tail), :], e_buf[slot, pl.ds(0, tail), :], 0, 0)
        to_top = push(dn_send, dn_half, p_send.at[2], p_recv.at[2], {'pp': partner})

        @pl.when(jnp.logical_and(is_top, jnp.logical_not(is_last)))
        def _():
            for k in range(num_tp):
                dn_send[k] = dn_acc[k * seq:(k + 1) * seq, :].astype(BF16)
            to_top.start()

        @pl.when(is_last)
        def _():
            to_top.wait_recv()
            for k in range(num_tp):
                both = dn_acc[k * seq:(k + 1) * seq, :] + dn_half[k].astype(F32)
                dn_acc[k * seq:(k + 1) * seq, :] = both
                dn_send[k] = both.astype(BF16)
            swap(DN, lambda peer: dn_send.at[peer], dn_recv, 'start')
            swap(DN, None, dn_recv, 'recv')
            grad_n = dn_acc[pl.ds(pl.multiple_of(rank * seq, seq), seq), :]
            for k in range(1, num_tp):
                grad_n = grad_n + dn_recv[lax.rem(rank + k, num_tp)].astype(F32)
            inv_rms, unit = norm_of()
            dy_in[0] = (inv_rms * (grad_n - unit * jnp.mean(unit * grad_n, axis=-1, keepdims=True))).astype(BF16)

    pl.run_scoped(grads_pass, pltpu.VMEM((2, tile, dim), BF16), pltpu.VMEM((num_tok, dim), F32))

    @pl.when(jnp.logical_not(is_last))
    def _():
        bwd.wait_recv()

    dy_all[rank] = dy_in[0]
    swap(DY, lambda peer: dy_in.at[0], dy_all, 'start')
    grad_y = dy_in[0]
    total = grad_y.astype(F32)
    for blk in range(num_tp):
        grad_h = (slope[blk] * dot_of(grad_y, w2s[blk], 1, 1)).astype(BF16)
        dh_own[blk] = grad_h
        total = total + dot_of(grad_h, w1s[blk], 1, 1)
    y_buf[1] = total.astype(BF16)

    @pl.when(jnp.logical_not(is_first))
    def _():
        bwd.start()

    @pl.when(is_first)
    def _():
        dx_all[rank] = y_buf[1]
        swap(DX, lambda peer: y_buf.at[1], dx_all, 'start')

    dh_cols[rank] = dh_own[rank]
    swap(DH, lambda peer: dh_own.at[peer], dh_cols, 'start')

    tree(DX, 1, dx_all, 0, 'start')
    out_copy(1).start()
    for idx, kind, dst in ((2, XA, x_all), (3, AC, a_cols), (4, DY, dy_all), (5, DH, dh_cols)):
        swap(kind, None, dst, 'recv')
        out_copy(idx).start()

    for idx in range(6):
        w_copy(idx).wait_send()

    @pl.when(is_first)
    def _():
        swap(X0, lambda peer: x0.at[peer], x0r, 'sent')
        swap(DX, lambda peer: y_buf.at[1], dx_all, 'sent')

    @pl.when(is_last)
    def _():
        swap(N, lambda peer: n_all.at[rank], n_all, 'sent')
        swap(DN, lambda peer: dn_send.at[peer], dn_recv, 'sent')

    @pl.when(jnp.logical_and(is_top, jnp.logical_not(is_last)))
    def _():
        push(dn_send, dn_half, p_send.at[2], p_recv.at[2], {'pp': partner}).wait_send()

    @pl.when(jnp.logical_not(is_last))
    def _():
        fwd.wait_send()

    @pl.when(jnp.logical_not(is_first))
    def _():
        bwd.wait_send()
    swap(XA, lambda peer: x_in.at[0], x_all, 'sent')
    swap(AC, lambda peer: a_own.at[peer], a_cols, 'sent')
    swap(DY, lambda peer: dy_in.at[0], dy_all, 'sent')
    swap(DH, lambda peer: dh_own.at[peer], dh_cols, 'sent')
    stats_swap('sent')
    tree(N, 0, n_all, last, 'sent')
    tree(DX, 1, dx_all, 0, 'sent')

    final = half - 1
    their_base = (1 - core) * (half * tile)

    @pl.when(is_odd)
    def _():
        if final >= 1:
            g_wait(final - 1, base0 + (final - 1) * tile, tile, (final - 1) % 2)
        g_wait(final, tail_base, tail, final % 2)

    @pl.when(jnp.logical_not(is_odd))
    def _():
        for i in range(max(final - 1, 0), half):
            g_wait(i, base0 + i * tile, tile, i % 2)
    for i in range(final):
        g_copies(i, their_base + i * tile, tile, i % 2)[1].wait_recv()

    @pl.when(is_odd)
    def _():
        g_copies(final, their_base + final * tile, tile, final % 2)[1].wait_recv()

    @pl.when(jnp.logical_not(is_odd))
    def _():
        g_copies(final, tail_base, tail, final % 2)[1].wait_recv()
    for idx in range(6):
        out_copy(idx).wait()


def table_kernel(block, meta, loss_in, n_all, dx_all, g_ref, xa, ac, dy, dh, loss_o, out_ref, dw1_o, dw2_o, dx_wide, acts, dw, sems):
    i = pl.program_id(0)
    num_tok, dim = dx_all.shape
    loads = [pltpu.make_async_copy(src, acts.at[j], sems.at[j]) for j, src in enumerate((ac, dy, xa, dh))]
    stores = [pltpu.make_async_copy(dw.at[j], dst, sems.at[4 + j]) for j, dst in enumerate((dw2_o, dw1_o))]

    @pl.when(i == 0)
    def _():
        for load in loads:
            load.start()
        dx_wide[...] = dx_all[...].astype(F32)
        loss_o[0] = jnp.max(loss_in[...])

    out_ref[...] = dot_of(g_ref[...], n_all[...], 1, 0)

    def add(k, carry):
        row = meta[0, k] - i * block
        out_ref[pl.ds(row, 1), :] += dx_wide[pl.ds(meta[1, k], 1), :]
        return carry
    lax.fori_loop(meta[2, i], meta[2, i + 1], add, 0)

    for j in range(2):
        @pl.when(i == 1 + j)
        def _():
            loads[2 * j].wait()
            loads[2 * j + 1].wait()
            dw[j] = dot_of(acts[2 * j], acts[2 * j + 1], 0, 0)
            stores[j].start()

    @pl.when(i == pl.num_programs(0) - 1)
    def _():
        for store in stores:
            store.wait()


def solution(mesh):
    num_tp, num_pp = mesh.shape['tp'], mesh.shape['pp']

    def device_fn(tokens, labels, emb_table, w_in, w_out):
        num_micro, seq = tokens.shape
        vocab, dim = emb_table.shape
        cols = w_in.shape[2]
        num_tok = num_micro * seq
        chunk = row_chunk(vocab)
        chunks = vocab // chunk
        half = 6 if chunks >= 60 else 2
        tile = chunk * pl.cdiv(chunks, 2 * half)
        vmem, hbm = pl.BlockSpec(memory_space=pltpu.VMEM), pl.BlockSpec(memory_space=pl.ANY)
        act = (num_tp, seq, dim)
        wide = (num_tp, seq, cols)
        shape = jax.ShapeDtypeStruct
        dma = pltpu.SemaphoreType.DMA
        loss, meta, g_all, n_all, dx_all, x_all, a_cols, dy_all, dh_cols = pl.pallas_call(
            functools.partial(step_kernel, num_tp, num_pp, tile, half),
            out_shape=(shape((8, 128), F32), shape((8, num_tok), jnp.int32), shape((vocab, num_tok), BF16),
                       shape(act, BF16), shape(act, BF16), shape(act, BF16), shape(wide, BF16), shape(act, BF16), shape(wide, BF16)),
            in_specs=[vmem, vmem, hbm, hbm, hbm],
            out_specs=(vmem, vmem, hbm, hbm, hbm, hbm, hbm, hbm, hbm),
            scratch_shapes=[
                pltpu.VMEM(act, BF16), pltpu.VMEM(act, BF16), pltpu.VMEM((num_tp, dim, cols), BF16), pltpu.VMEM((num_tp, cols, dim), BF16),
                pltpu.VMEM((1, seq, dim), BF16), pltpu.VMEM((2, seq, dim), BF16), pltpu.VMEM(wide, BF16), pltpu.VMEM(wide, F32),
                pltpu.VMEM(act, BF16), pltpu.VMEM(act, BF16), pltpu.VMEM(wide, BF16), pltpu.VMEM(act, BF16), pltpu.VMEM(wide, BF16),
                pltpu.VMEM(wide, BF16), pltpu.VMEM((1, seq, dim), BF16), pltpu.VMEM(act, BF16),
                pltpu.VMEM((half * tile, num_tok), F32), pltpu.VMEM((2 * num_tp, 8, num_tok), F32),
                pltpu.VMEM(act, BF16), pltpu.VMEM(act, BF16), pltpu.VMEM(act, BF16),
                pltpu.VMEM((2, tile, num_tok), BF16), pltpu.VMEM((num_tok, 128), F32),
                dma((6,)), dma((6,)), dma((3,)), dma((3,)), dma((8, num_tp)), dma((8, num_tp)), dma((2, 3, num_tp)),
                dma((2 * num_tp,)), dma((2 * num_tp,)), dma((2,)), dma((half,)), dma((6,)), dma((6,)),
            ],
            compiler_params=pltpu.CompilerParams(collective_id=0, has_side_effects=True, vmem_limit_bytes=67043328),
            name='step_kernel',
        )(tokens.reshape(1, num_tok), labels.reshape(1, num_tok), emb_table, w_in[0], w_out[0])

        whole = lambda shp: pl.BlockSpec(shp, lambda i, meta: (0, 0))
        flat = lambda arr: arr.reshape(num_tok, arr.shape[2])
        loss, grad_table, grad_one, grad_two = pl.pallas_call(
            functools.partial(table_kernel, tile),
            grid_spec=pltpu.PrefetchScalarGridSpec(
                num_scalar_prefetch=1,
                grid=(pl.cdiv(vocab, tile),),
                in_specs=[whole((8, 128)), whole((num_tok, dim)), whole((num_tok, dim)), pl.BlockSpec((tile, num_tok), lambda i, meta: (i, 0)), hbm, hbm, hbm, hbm],
                out_specs=(pl.BlockSpec(memory_space=pltpu.SMEM), pl.BlockSpec((tile, dim), lambda i, meta: (i, 0)), hbm, hbm),
                scratch_shapes=[pltpu.VMEM((num_tok, dim), F32), pltpu.VMEM((4, num_tok, dim), BF16), pltpu.VMEM((2, dim, dim), F32), dma((6,))],
            ),
            out_shape=(shape((1,), F32), shape((vocab, dim), F32), shape((dim, cols), F32), shape((cols, dim), F32)),
            compiler_params=pltpu.CompilerParams(dimension_semantics=('arbitrary',), vmem_limit_bytes=67043328),
            name='table_kernel',
        )(meta, loss, flat(n_all), flat(dx_all), g_all, flat(x_all), flat(a_cols), flat(dy_all), flat(dh_cols))
        return loss, grad_one[None], grad_two[None], grad_table

    return jax.shard_map(device_fn, mesh=mesh, in_specs=(P('dp', None), P('dp', None), P('tp', None), P('pp', None, 'tp'), P('pp', 'tp', None)), out_specs=(P('dp'), P(('dp', 'pp'), None, 'tp'), P(('dp', 'pp'), 'tp', None), P(('dp', 'tp'), None)), check_vma=False)
```

time: 315 us -> 272 us (0.86)
  the two profiles are of different devices: /device:TPU:96 before, /device:TPU:101 now
where the time goes in v3:
time: 272 us; the launch traced here: 271 us
  Pallas kernels  270 us (99%)
    pallas_call x1, Pallas kernels, device_fn(): pl.pallas_call(functools.partial(step_kernel, num_tp, num_pp, tile, half)...  245 us
    pallas_call x1, Pallas kernels, device_fn(): pl.pallas_call(functools.partial(table_kernel, tile), grid_spec=pltpu.Pre...  25.3 us

profile of v3, /device:TPU:101, one launch (start us, length us, event | category | flops | bytes accessed | tf_op | source)
XLA Modules:
  0.0 271.0 jit_solution(3459129845477972098)
XLA Ops:
  0.6 245.0 %step_kernel.1 = (f32[8,128]{1,0:T(8,128)}, s32[8,512]{1,0:T(8,128)}, bf16[12576,512]{1,0:T(8,128)(2,1)}, bf16[4,128,768]{2,1,0:T(8,128)(2,1)}, bf16[4,128,768]{...) custom-call(s32[1,512]{1,0:T(1,128)} %bitcast.20, ...), custom_call_target="tpu_custom_call" | custom-call | tf_op jit(solution)/shard_map/step_kernel/pallas_call | solution.py:590
  245.6 25.3 %table_kernel.1 = (f32[1]{0:T(128)}, f32[12576,768]{1,0:T(8,128)}, f32[768,768]{1,0:T(8,128)}, f32[768,768]{1,0:T(8,128)}) custom-call(s32[8,512]{1,0:T(8,128)} %get-tuple-element.17.meta, f32[8,128]{1,0:T(8,128)} %get-tuple-element.18.loss_in, bf16[512,768]{1,0:T(8,128)(2,1)} %bitcast.14, bf16[512,768]{1,0:T(8,128)(2,1)} %bitcast.15, ...), custom_call_target="tpu_custom_call" | custom-call | tf_op jit(solution)/shard_map/table_kernel/pallas_call | solution.py:613

commit v4 on v3

--- a/solution.py
+++ b/solution.py
@@ -33,7 +33,7 @@
 
 def step_kernel(num_tp, num_pp, tile, half, tok, lab, e_hbm, w1_hbm, w2_hbm,
                 loss_o, meta_o, g_o, n_o, dx_o, xa_o, ac_o, dy_o, dh_o,
-                x0, x0r, w1s, w2s, x_in, y_buf, a_own, slope, n_all, x_all, a_cols, dy_all, dh_cols, dh_own, dy_in, dx_all,
+                x0, x0r, w1s, w2s, w1t, w2t, x_in, y_buf, a_own, slope, n_all, x_all, a_cols, dy_all, dh_cols, dh_own, dy_in, dx_all,
                 logit, stat, dn_send, dn_recv, dn_half, g_buf, key_buf,
                 w_send, w_recv, p_send, p_recv, tp_send, tp_recv, tree_send, st_send, st_recv, g_send, g_recv, out_sem, loc):
     rank = lax.axis_index('tp')
@@ -125,6 +125,13 @@
     for idx in (0, 3, 1, 2):
         w_copy(idx).start()
 
+    def flip(src, dst, who):
+        def one(j, carry):
+            part = pl.ds(pl.multiple_of(j * 128, 128), 128)
+            dst[who, :, part] = jnp.transpose(src[who, part, :])
+            return carry
+        lax.fori_loop(0, src.shape[1] // 128, one, 0)
+
     num_tok = num_tp * seq
     vocab_base = rank * vocab
     tail_base = (2 * half - 1) * tile
@@ -210,10 +217,16 @@
         pl.run_scoped(lookup_pass, pltpu.VMEM((2, tile, dim), BF16), pltpu.VMEM((num_tok, dim), F32))
         swap(X0, lambda peer: x0.at[peer], x0r, 'start')
 
+    own1.wait()
+    own2.wait()
+    flip(w1s, w1t, rank)
+    flip(w2s, w2t, rank)
     w_wait(0)
     w_copy(4).start()
     w_wait(3)
     w_copy(5).start()
+    flip(w1s, w1t, left)
+    flip(w2s, w2t, right)
 
     @pl.when(is_first)
     def _():
@@ -223,30 +236,52 @@
             total = total + x0r[lax.rem(rank + k, num_tp)].astype(F32)
         x_in[0] = total.astype(BF16)
 
-    for idx in (1, 2, 4, 5):
-        w_wait(idx)
-    own1.wait()
-    own2.wait()
-
-    fwd = push(y_buf.at[0], x_in.at[0], p_send.at[0], p_recv.at[0], {'pp': jnp.minimum(stage + 1, last)})
-    bwd = push(y_buf.at[1], dy_in.at[0], p_send.at[1], p_recv.at[1], {'pp': jnp.maximum(stage - 1, 0)})
+    w_wait(1)
+    w_wait(2)
+    flip(w2s, w2t, left)
+    flip(w1s, w1t, right)
+    w_wait(4)
+    w_wait(5)
+
+    cols = w1s.shape[2]
+    piece = 256 if cols % 256 == 0 and dim % 256 == 0 else 128
+    cut = dim // 3 // 128 * 128
+    spans = [(0, cut), (cut, dim - cut)] if cut else [(0, dim)]
+
+    def hop(kind, src, dst, part, dest):
+        lo, size = spans[part]
+        view = (0, slice(None), pl.ds(lo, size))
+        return push(src.at[view], dst.at[view], p_send.at[2 * kind + part], p_recv.at[2 * kind + part], {'pp': dest})
+
+    def hops(kind, mode):
+        src, dst = (y_buf.at[pl.ds(0, 1)], x_in) if kind == 0 else (y_buf.at[pl.ds(1, 1)], dy_in)
+        dest = jnp.minimum(stage + 1, last) if kind == 0 else jnp.maximum(stage - 1, 0)
+        return [hop(kind, src, dst, part, dest) for part in range(len(spans))]
+
+    def send_rows(kind, source, acts, mats, active):
+        for part, (lo, size) in enumerate(spans):
+            for off in range(lo, lo + size, piece):
+                total = source[0, :, off:off + piece].astype(F32)
+                for blk in range(num_tp):
+                    total = total + dot_of(acts[blk], mats[blk, :, off:off + piece], 1, 0)
+                y_buf[kind, :, off:off + piece] = total.astype(BF16)
+
+            @pl.when(active)
+            def _():
+                hops(kind, 'start')[part].start()
 
     @pl.when(jnp.logical_not(is_first))
     def _():
-        fwd.wait_recv()
+        for copy in hops(0, 'recv'):
+            copy.wait_recv()
 
     x_act = x_in[0]
-    total = x_act.astype(F32)
     for blk in range(num_tp):
-        gate, grad = gelu_pair(dot_of(x_act, w1s[blk], 1, 0))
-        a_own[blk] = gate.astype(BF16)
-        slope[blk] = grad
-        total = total + dot_of(a_own[blk], w2s[blk], 1, 0)
-    y_buf[0] = total.astype(BF16)
-
-    @pl.when(jnp.logical_not(is_last))
-    def _():
-        fwd.start()
+        for off in range(0, cols, piece):
+            gate, grad = gelu_pair(dot_of(x_act, w1s[blk, :, off:off + piece], 1, 0))
+            a_own[blk, :, off:off + piece] = gate.astype(BF16)
+            slope[blk, :, off:off + piece] = grad
+    send_rows(0, x_in, a_own, w2s, jnp.logical_not(is_last))
 
     def norm_of():
         wide = y_buf[0].astype(F32)
@@ -258,6 +293,8 @@
         n_all[rank] = norm_of()[1].astype(BF16)
         swap(N, lambda peer: n_all.at[rank], n_all, 'start')
 
+    flip(w1s, w1t, opp)
+    flip(w2s, w2t, opp)
     tree(N, 0, n_all, last, 'start')
     x_all[rank] = x_in[0]
     a_cols[rank] = a_own[rank]
@@ -419,7 +456,7 @@
             def _():
                 fetch(e_buf, tail_base, tail, slot).wait()
                 dn_acc[...] += dot_of(g_buf[slot, pl.ds(0, tail), :], e_buf[slot, pl.ds(0, tail), :], 0, 0)
-        to_top = push(dn_send, dn_half, p_send.at[2], p_recv.at[2], {'pp': partner})
+        to_top = push(dn_send, dn_half, p_send.at[4], p_recv.at[4], {'pp': partner})
 
         @pl.when(jnp.logical_and(is_top, jnp.logical_not(is_last)))
         def _():
@@ -446,21 +483,17 @@
 
     @pl.when(jnp.logical_not(is_last))
     def _():
-        bwd.wait_recv()
+        for copy in hops(1, 'recv'):
+            copy.wait_recv()
 
     dy_all[rank] = dy_in[0]
     swap(DY, lambda peer: dy_in.at[0], dy_all, 'start')
     grad_y = dy_in[0]
-    total = grad_y.astype(F32)
     for blk in range(num_tp):
-        grad_h = (slope[blk] * dot_of(grad_y, w2s[blk], 1, 1)).astype(BF16)
-        dh_own[blk] = grad_h
-        total = total + dot_of(grad_h, w1s[blk], 1, 1)
-    y_buf[1] = total.astype(BF16)
-
-    @pl.when(jnp.logical_not(is_first))
-    def _():
-        bwd.start()
+        for off in range(0, cols, piece):
+            grad_a = dot_of(grad_y, w2t[blk, :, off:off + piece], 1, 0)
+            dh_own[blk, :, off:off + piece] = (slope[blk, :, off:off + piece] * grad_a).astype(BF16)
+    send_rows(1, dy_in, dh_own, w1t, jnp.logical_not(is_first))
 
     @pl.when(is_first)
     def _():
@@ -468,9 +501,17 @@
         swap(DX, lambda peer: y_buf.at[1], dx_all, 'start')
 
     dh_cols[rank] = dh_own[rank]
-    swap(DH, lambda peer: dh_own.at[peer], dh_cols, 'start')
+
+    @pl.when(chip != 0)
+    def _():
+        swap(DH, lambda peer: dh_own.at[peer], dh_cols, 'start')
 
     tree(DX, 1, dx_all, 0, 'start')
+
+    @pl.when(chip == 0)
+    def _():
+        swap(DH, lambda peer: dh_own.at[peer], dh_cols, 'start')
+
     out_copy(1).start()
     for idx, kind, dst in ((2, XA, x_all), (3, AC, a_cols), (4, DY, dy_all), (5, DH, dh_cols)):
         swap(kind, None, dst, 'recv')
@@ -491,15 +532,17 @@
 
     @pl.when(jnp.logical_and(is_top, jnp.logical_not(is_last)))
     def _():
-        push(dn_send, dn_half, p_send.at[2], p_recv.at[2], {'pp': partner}).wait_send()
+        push(dn_send, dn_half, p_send.at[4], p_recv.at[4], {'pp': partner}).wait_send()
 
     @pl.when(jnp.logical_not(is_last))
     def _():
-        fwd.wait_send()
+        for copy in hops(0, 'sent'):
+            copy.wait_send()
 
     @pl.when(jnp.logical_not(is_first))
     def _():
-        bwd.wait_send()
+        for copy in hops(1, 'sent'):
+            copy.wait_send()
     swap(XA, lambda peer: x_in.at[0], x_all, 'sent')
     swap(AC, lambda peer: a_own.at[peer], a_cols, 'sent')
     swap(DY, lambda peer: dy_in.at[0], dy_all, 'sent')
@@ -595,13 +638,14 @@
             out_specs=(vmem, vmem, hbm, hbm, hbm, hbm, hbm, hbm, hbm),
             scratch_shapes=[
                 pltpu.VMEM(act, BF16), pltpu.VMEM(act, BF16), pltpu.VMEM((num_tp, dim, cols), BF16), pltpu.VMEM((num_tp, cols, dim), BF16),
+                pltpu.VMEM((num_tp, cols, dim), BF16), pltpu.VMEM((num_tp, dim, cols), BF16),
                 pltpu.VMEM((1, seq, dim), BF16), pltpu.VMEM((2, seq, dim), BF16), pltpu.VMEM(wide, BF16), pltpu.VMEM(wide, F32),
                 pltpu.VMEM(act, BF16), pltpu.VMEM(act, BF16), pltpu.VMEM(wide, BF16), pltpu.VMEM(act, BF16), pltpu.VMEM(wide, BF16),
                 pltpu.VMEM(wide, BF16), pltpu.VMEM((1, seq, dim), BF16), pltpu.VMEM(act, BF16),
                 pltpu.VMEM((half * tile, num_tok), F32), pltpu.VMEM((2 * num_tp, 8, num_tok), F32),
                 pltpu.VMEM(act, BF16), pltpu.VMEM(act, BF16), pltpu.VMEM(act, BF16),
                 pltpu.VMEM((2, tile, num_tok), BF16), pltpu.VMEM((num_tok, 128), F32),
-                dma((6,)), dma((6,)), dma((3,)), dma((3,)), dma((8, num_tp)), dma((8, num_tp)), dma((2, 3, num_tp)),
+                dma((6,)), dma((6,)), dma((5,)), dma((5,)), dma((8, num_tp)), dma((8, num_tp)), dma((2, 3, num_tp)),
                 dma((2 * num_tp,)), dma((2 * num_tp,)), dma((2,)), dma((half,)), dma((6,)), dma((6,)),
             ],
             compiler_params=pltpu.CompilerParams(collective_id=0, has_side_effects=True, vmem_limit_bytes=67043328),

time: 272 us -> 254 us (0.934)
  the two profiles are of different devices: /device:TPU:101 before, /device:TPU:97 now
where the time goes in v4:
time: 254 us; the launch traced here: 253 us
  Pallas kernels  252 us (99%)
    pallas_call x1, Pallas kernels, device_fn(): pl.pallas_call(functools.partial(step_kernel, num_tp, num_pp, tile, half)...  227 us
    pallas_call x1, Pallas kernels, device_fn(): pl.pallas_call(functools.partial(table_kernel, tile), grid_spec=pltpu.Pre...  25.1 us

profile of v4, /device:TPU:97, one launch (start us, length us, event | category | flops | bytes accessed | tf_op | source)
XLA Modules:
  0.0 252.8 jit_solution(11412231712509047)
XLA Ops:
  0.6 226.9 %step_kernel.1 = (f32[8,128]{1,0:T(8,128)}, s32[8,512]{1,0:T(8,128)}, bf16[12576,512]{1,0:T(8,128)(2,1)}, bf16[4,128,768]{2,1,0:T(8,128)(2,1)}, bf16[4,128,768]{...) custom-call(s32[1,512]{1,0:T(1,128)} %bitcast.20, ...), custom_call_target="tpu_custom_call" | custom-call | tf_op jit(solution)/shard_map/step_kernel/pallas_call | solution.py:633
  227.5 25.1 %table_kernel.1 = (f32[1]{0:T(128)}, f32[12576,768]{1,0:T(8,128)}, f32[768,768]{1,0:T(8,128)}, f32[768,768]{1,0:T(8,128)}) custom-call(s32[8,512]{1,0:T(8,128)} %get-tuple-element.17.meta, f32[8,128]{1,0:T(8,128)} %get-tuple-element.18.loss_in, bf16[512,768]{1,0:T(8,128)(2,1)} %bitcast.14, bf16[512,768]{1,0:T(8,128)(2,1)} %bitcast.15, ...), custom_call_target="tpu_custom_call" | custom-call | tf_op jit(solution)/shard_map/table_kernel/pallas_call | solution.py:657

commit v5 on v4

--- a/solution.py
+++ b/solution.py
@@ -34,8 +34,8 @@
 def step_kernel(num_tp, num_pp, tile, half, tok, lab, e_hbm, w1_hbm, w2_hbm,
                 loss_o, meta_o, g_o, n_o, dx_o, xa_o, ac_o, dy_o, dh_o,
                 x0, x0r, w1s, w2s, w1t, w2t, x_in, y_buf, a_own, slope, n_all, x_all, a_cols, dy_all, dh_cols, dh_own, dy_in, dx_all,
-                logit, stat, dn_send, dn_recv, dn_half, g_buf, key_buf,
-                w_send, w_recv, p_send, p_recv, tp_send, tp_recv, tree_send, st_send, st_recv, g_send, g_recv, out_sem, loc):
+                logit, stat, dn_send, dn_recv, dn_half, g_buf, key_buf, via_x, via_y,
+                w_send, w_recv, p_send, p_recv, tp_send, tp_recv, tree_send, st_send, st_recv, g_send, g_recv, out_sem, loc, via_send, via_recv):
     rank = lax.axis_index('tp')
     stage = lax.axis_index('pp')
     last = num_pp - 1
@@ -65,6 +65,8 @@
     chip, core = stage // 2, lax.rem(stage, 2)
     partner = chip * 2 + 1 - core
     is_top = chip == num_x - 1
+    is_lookup = stage == last - 1
+    mirror = (num_x - 1 - chip) * 2 + core
 
     def tree(kind, tid, buf, root, mode):
         root_x, root_c = root // 2, root % 2
@@ -112,18 +114,74 @@
     own1.start()
     own2.start()
 
-    def w_copy(idx):
+    rows_w = w1_hbm.shape[0]
+    detours = [(0, rows_w // 2), (1, rows_w // 4)] if num_x >= 4 else []
+
+    def w_copy(idx, rows=None):
         src, full, who, dev = [
             (w1_hbm, w1s, rank, right), (w2_hbm, w2s, rank, right), (w1_hbm, w1s, rank, left), (w2_hbm, w2s, rank, left),
             (w1s.at[left], w1s, left, right), (w2s.at[right], w2s, right, left)][idx]
-        return push(src, full.at[who], w_send.at[idx], w_recv.at[idx], {'tp': dev})
-
-    def w_wait(idx):
+        if rows is None:
+            return push(src, full.at[who], w_send.at[idx], w_recv.at[idx], {'tp': dev})
+        part = pl.ds(0, rows)
+        return push(src.at[part], full.at[who, part], w_send.at[idx], w_recv.at[idx], {'tp': dev})
+
+    def w_wait(idx, rows=None):
         full, who = [(w1s, left), (w2s, left), (w1s, right), (w2s, right), (w1s, opp), (w2s, opp)][idx]
-        push(full.at[who], full.at[who], w_send.at[idx], w_recv.at[idx], {'tp': rank}).wait_recv()
-
-    for idx in (0, 3, 1, 2):
-        w_copy(idx).start()
+        view = full.at[who] if rows is None else full.at[who, pl.ds(0, rows)]
+        push(view, view, w_send.at[idx], w_recv.at[idx], {'tp': rank}).wait_recv()
+
+    def by_chip(action):
+        for near, size in detours:
+            pl.when(chip == near)(functools.partial(action, rows_w - size))
+        pl.when(chip >= len(detours))(functools.partial(action, None))
+
+    def detour(size, leg, j):
+        part = pl.ds(0, size)
+        tail_rows = pl.ds(rows_w - size, size)
+        if leg == 0:
+            src = (w2_hbm, w1_hbm)[j].at[tail_rows]
+            return push(src, via_x.at[j, part], via_send.at[j], via_recv.at[j], {'pp': mirror})
+        if leg == 1:
+            return push(via_x.at[j, part], via_y.at[j, part], via_send.at[2 + j], via_recv.at[2 + j], {'tp': (right, left)[j]})
+        full, who = ((w2s, left), (w1s, right))[j]
+        return push(via_y.at[j, part], full.at[who, tail_rows], via_send.at[4 + j], via_recv.at[4 + j], {'pp': mirror})
+
+    def on_detour(helper, action):
+        for near, size in detours:
+            pl.when(chip == (num_x - 1 - near if helper else near))(functools.partial(action, size))
+
+    w_copy(0).start()
+    w_copy(3).start()
+
+    def leave(size):
+        for j in range(2):
+            detour(size, 0, j).start()
+
+    def pass_on(size):
+        for j in range(2):
+            detour(size, 0, j).wait_recv()
+            detour(size, 1, j).start()
+
+    def bring_back(size):
+        for j in range(2):
+            detour(size, 1, j).wait_recv()
+            detour(size, 2, j).start()
+
+    def arrive(size):
+        for j in range(2):
+            detour(size, 2, j).wait_recv()
+
+    def second(rows):
+        w_copy(1, rows).start()
+        w_copy(2, rows).start()
+
+    on_detour(False, leave)
+    on_detour(True, pass_on)
+
+    @pl.when(jnp.logical_not(is_lookup))
+    def _():
+        by_chip(second)
 
     def flip(src, dst, who):
         def one(j, carry):
@@ -212,10 +270,23 @@
         for k in range(num_tp):
             x0[k] = acc[k * seq:(k + 1) * seq, :].astype(BF16)
 
-    @pl.when(is_first)
+    @pl.when(is_lookup)
     def _():
         pl.run_scoped(lookup_pass, pltpu.VMEM((2, tile, dim), BF16), pltpu.VMEM((num_tok, dim), F32))
         swap(X0, lambda peer: x0.at[peer], x0r, 'start')
+        second(None)
+
+    on_detour(True, bring_back)
+    first_x = push(y_buf.at[pl.ds(1, 1)], x_in, p_send.at[5], p_recv.at[5], {'pp': 0})
+
+    @pl.when(is_lookup)
+    def _():
+        swap(X0, None, x0r, 'recv')
+        total = x0[rank].astype(F32)
+        for k in range(1, num_tp):
+            total = total + x0r[lax.rem(rank + k, num_tp)].astype(F32)
+        y_buf[1] = total.astype(BF16)
+        first_x.start()
 
     own1.wait()
     own2.wait()
@@ -228,16 +299,16 @@
     flip(w1s, w1t, left)
     flip(w2s, w2t, right)
 
-    @pl.when(is_first)
-    def _():
-        swap(X0, None, x0r, 'recv')
-        total = x0[rank].astype(F32)
-        for k in range(1, num_tp):
-            total = total + x0r[lax.rem(rank + k, num_tp)].astype(F32)
-        x_in[0] = total.astype(BF16)
-
-    w_wait(1)
-    w_wait(2)
+    @pl.when(is_lookup)
+    def _():
+        first_x.wait_send()
+
+    def second_in(rows):
+        w_wait(1, rows)
+        w_wait(2, rows)
+
+    by_chip(second_in)
+    on_detour(False, arrive)
     flip(w2s, w2t, left)
     flip(w1s, w1t, right)
     w_wait(4)
@@ -274,6 +345,10 @@
     def _():
         for copy in hops(0, 'recv'):
             copy.wait_recv()
+
+    @pl.when(is_first)
+    def _():
+        first_x.wait_recv()
 
     x_act = x_in[0]
     for blk in range(num_tp):
@@ -517,12 +592,32 @@
         swap(kind, None, dst, 'recv')
         out_copy(idx).start()
 
-    for idx in range(6):
+    for idx in (0, 3, 4, 5):
         w_copy(idx).wait_send()
 
+    def second_sent(rows):
+        w_copy(1, rows).wait_send()
+        w_copy(2, rows).wait_send()
+
+    def left_sent(size):
+        for j in range(2):
+            detour(size, 0, j).wait_send()
+
+    def help_sent(size):
+        for j in range(2):
+            detour(size, 1, j).wait_send()
+            detour(size, 2, j).wait_send()
+
+    by_chip(second_sent)
+    on_detour(False, left_sent)
+    on_detour(True, help_sent)
+
+    @pl.when(is_lookup)
+    def _():
+        swap(X0, lambda peer: x0.at[peer], x0r, 'sent')
+
     @pl.when(is_first)
     def _():
-        swap(X0, lambda peer: x0.at[peer], x0r, 'sent')
         swap(DX, lambda peer: y_buf.at[1], dx_all, 'sent')
 
     @pl.when(is_last)
@@ -645,8 +740,9 @@
                 pltpu.VMEM((half * tile, num_tok), F32), pltpu.VMEM((2 * num_tp, 8, num_tok), F32),
                 pltpu.VMEM(act, BF16), pltpu.VMEM(act, BF16), pltpu.VMEM(act, BF16),
                 pltpu.VMEM((2, tile, num_tok), BF16), pltpu.VMEM((num_tok, 128), F32),
-                dma((6,)), dma((6,)), dma((5,)), dma((5,)), dma((8, num_tp)), dma((8, num_tp)), dma((2, 3, num_tp)),
-                dma((2 * num_tp,)), dma((2 * num_tp,)), dma((2,)), dma((half,)), dma((6,)), dma((6,)),
+                pltpu.VMEM((2, dim // 2, dim), BF16), pltpu.VMEM((2, dim // 2, dim), BF16),
+                dma((6,)), dma((6,)), dma((6,)), dma((6,)), dma((8, num_tp)), dma((8, num_tp)), dma((2, 3, num_tp)),
+                dma((2 * num_tp,)), dma((2 * num_tp,)), dma((2,)), dma((half,)), dma((6,)), dma((6,)), dma((6,)), dma((6,)),
             ],
             compiler_params=pltpu.CompilerParams(collective_id=0, has_side_effects=True, vmem_limit_bytes=67043328),
             name='step_kernel',

time: 254 us -> 242 us (0.953)
  Pallas kernels: 252 us -> 240 us
    pallas_call x1, Pallas kernels: 227 us -> 215 us  [device_fn(): pl.pallas_call(functools.partial(step_kernel, num_tp, num_pp, tile, half)...]
where the time goes in v5:
time: 242 us; the launch traced here: 241 us
  Pallas kernels  240 us (99%)
    pallas_call x1, Pallas kernels, device_fn(): pl.pallas_call(functools.partial(step_kernel, num_tp, num_pp, tile, half)...  215 us
    pallas_call x1, Pallas kernels, device_fn(): pl.pallas_call(functools.partial(table_kernel, tile), grid_spec=pltpu.Pre...  25.3 us

profile of v5, /device:TPU:97, one launch (start us, length us, event | category | flops | bytes accessed | tf_op | source)
XLA Modules:
  0.0 241.2 jit_solution(1586496982616692084)
XLA Ops:
  0.6 215.2 %step_kernel.1 = (f32[8,128]{1,0:T(8,128)}, s32[8,512]{1,0:T(8,128)}, bf16[12576,512]{1,0:T(8,128)(2,1)}, bf16[4,128,768]{2,1,0:T(8,128)(2,1)}, bf16[4,128,768]{...) custom-call(s32[1,512]{1,0:T(1,128)} %bitcast.20, ...), custom_call_target="tpu_custom_call" | custom-call | tf_op jit(solution)/shard_map/step_kernel/pallas_call | solution.py:728
  215.8 25.3 %table_kernel.1 = (f32[1]{0:T(128)}, f32[12576,768]{1,0:T(8,128)}, f32[768,768]{1,0:T(8,128)}, f32[768,768]{1,0:T(8,128)}) custom-call(s32[8,512]{1,0:T(8,128)} %get-tuple-element.17.meta, f32[8,128]{1,0:T(8,128)} %get-tuple-element.18.loss_in, bf16[512,768]{1,0:T(8,128)(2,1)} %bitcast.14, bf16[512,768]{1,0:T(8,128)(2,1)} %bitcast.15, ...), custom_call_target="tpu_custom_call" | custom-call | tf_op jit(solution)/shard_map/table_kernel/pallas_call | solution.py:753

commit v6 on v5

--- a/solution.py
+++ b/solution.py
@@ -31,7 +31,7 @@
     return hid * cdf, slope
 
 
-def step_kernel(num_tp, num_pp, tile, half, tok, lab, e_hbm, w1_hbm, w2_hbm,
+def step_kernel(num_tp, num_pp, tile, half, block, tok, lab, e_hbm, w1_hbm, w2_hbm,
                 loss_o, meta_o, g_o, n_o, dx_o, xa_o, ac_o, dy_o, dh_o,
                 x0, x0r, w1s, w2s, w1t, w2t, x_in, y_buf, a_own, slope, n_all, x_all, a_cols, dy_all, dh_cols, dh_own, dy_in, dx_all,
                 logit, stat, dn_send, dn_recv, dn_half, g_buf, key_buf, via_x, via_y,
@@ -115,7 +115,7 @@
     own2.start()
 
     rows_w = w1_hbm.shape[0]
-    detours = [(0, rows_w // 2), (1, rows_w // 4)] if num_x >= 4 else []
+    detours = [(0, rows_w * 3 // 8), (1, rows_w // 8)] if num_x >= 4 else []
 
     def w_copy(idx, rows=None):
         src, full, who, dev = [
@@ -218,7 +218,7 @@
 
         def starts(b, acc):
             here = key_buf[pl.ds(pl.multiple_of(b * step, step), step), 0:1]
-            return acc + jnp.sum(jnp.where(here < lanes * tile, 1.0, 0.0), axis=0, keepdims=True)
+            return acc + jnp.sum(jnp.where(here < lanes * block, 1.0, 0.0), axis=0, keepdims=True)
 
         zero = jnp.zeros((1, num_tok), F32)
         pos_row = lax.fori_loop(0, num_tok // step, count, zero)
@@ -373,8 +373,12 @@
     tree(N, 0, n_all, last, 'start')
     x_all[rank] = x_in[0]
     a_cols[rank] = a_own[rank]
-    swap(XA, lambda peer: x_in.at[0], x_all, 'start')
-    swap(AC, lambda peer: a_own.at[peer], a_cols, 'start')
+
+    @pl.when(jnp.logical_not(is_top))
+    def _():
+        swap(XA, lambda peer: x_in.at[0], x_all, 'start')
+        swap(AC, lambda peer: a_own.at[peer], a_cols, 'start')
+
     outs = [(n_all, n_o), (dx_all, dx_o), (x_all, xa_o), (a_cols, ac_o), (dy_all, dy_o), (dh_cols, dh_o)]
 
     def out_copy(idx):
@@ -453,6 +457,11 @@
 
     stats_swap('start')
     stats_swap('recv')
+
+    @pl.when(is_top)
+    def _():
+        swap(XA, lambda peer: x_in.at[0], x_all, 'start')
+
     peak = stat[0, 0:1, :]
     for j in range(1, 2 * num_tp):
         peak = jnp.maximum(peak, stat[j, 0:1, :])
@@ -570,6 +579,10 @@
             dh_own[blk, :, off:off + piece] = (slope[blk, :, off:off + piece] * grad_a).astype(BF16)
     send_rows(1, dy_in, dh_own, w1t, jnp.logical_not(is_first))
 
+    @pl.when(is_top)
+    def _():
+        swap(AC, lambda peer: a_own.at[peer], a_cols, 'start')
+
     @pl.when(is_first)
     def _():
         dx_all[rank] = y_buf[1]
@@ -720,13 +733,14 @@
         chunks = vocab // chunk
         half = 6 if chunks >= 60 else 2
         tile = chunk * pl.cdiv(chunks, 2 * half)
+        block = min(640, tile)
         vmem, hbm = pl.BlockSpec(memory_space=pltpu.VMEM), pl.BlockSpec(memory_space=pl.ANY)
         act = (num_tp, seq, dim)
         wide = (num_tp, seq, cols)
         shape = jax.ShapeDtypeStruct
         dma = pltpu.SemaphoreType.DMA
         loss, meta, g_all, n_all, dx_all, x_all, a_cols, dy_all, dh_cols = pl.pallas_call(
-            functools.partial(step_kernel, num_tp, num_pp, tile, half),
+            functools.partial(step_kernel, num_tp, num_pp, tile, half, block),
             out_shape=(shape((8, 128), F32), shape((8, num_tok), jnp.int32), shape((vocab, num_tok), BF16),
                        shape(act, BF16), shape(act, BF16), shape(act, BF16), shape(wide, BF16), shape(act, BF16), shape(wide, BF16)),
             in_specs=[vmem, vmem, hbm, hbm, hbm],
@@ -751,12 +765,12 @@
         whole = lambda shp: pl.BlockSpec(shp, lambda i, meta: (0, 0))
         flat = lambda arr: arr.reshape(num_tok, arr.shape[2])
         loss, grad_table, grad_one, grad_two = pl.pallas_call(
-            functools.partial(table_kernel, tile),
+            functools.partial(table_kernel, block),
             grid_spec=pltpu.PrefetchScalarGridSpec(
                 num_scalar_prefetch=1,
-                grid=(pl.cdiv(vocab, tile),),
-                in_specs=[whole((8, 128)), whole((num_tok, dim)), whole((num_tok, dim)), pl.BlockSpec((tile, num_tok), lambda i, meta: (i, 0)), hbm, hbm, hbm, hbm],
-                out_specs=(pl.BlockSpec(memory_space=pltpu.SMEM), pl.BlockSpec((tile, dim), lambda i, meta: (i, 0)), hbm, hbm),
+                grid=(pl.cdiv(vocab, block),),
+                in_specs=[whole((8, 128)), whole((num_tok, dim)), whole((num_tok, dim)), pl.BlockSpec((block, num_tok), lambda i, meta: (i, 0)), hbm, hbm, hbm, hbm],
+                out_specs=(pl.BlockSpec(memory_space=pltpu.SMEM), pl.BlockSpec((block, dim), lambda i, meta: (i, 0)), hbm, hbm),
                 scratch_shapes=[pltpu.VMEM((num_tok, dim), F32), pltpu.VMEM((4, num_tok, dim), BF16), pltpu.VMEM((2, dim, dim), F32), dma((6,))],
             ),
             out_shape=(shape((1,), F32), shape((vocab, dim), F32), shape((dim, cols), F32), shape((cols, dim), F32)),

time: 242 us -> 242 us (level)
  no operation moved by 1% of the time
where the time goes in v6:
time: 242 us; the launch traced here: 241 us
  Pallas kernels  240 us (99%)
    pallas_call x1, Pallas kernels, device_fn(): pl.pallas_call(functools.partial(step_kernel, num_tp, num_pp, tile, half,...  211 us
    pallas_call x1, Pallas kernels, device_fn(): pl.pallas_call(functools.partial(table_kernel, block), grid_spec=pltpu.Pr...  28.9 us

profile of v6, /device:TPU:97, one launch (start us, length us, event | category | flops | bytes accessed | tf_op | source)
XLA Modules:
  0.0 240.8 jit_solution(7147547825767223200)
XLA Ops:
  0.6 211.2 %step_kernel.1 = (f32[8,128]{1,0:T(8,128)}, s32[8,512]{1,0:T(8,128)}, bf16[12576,512]{1,0:T(8,128)(2,1)}, bf16[4,128,768]{2,1,0:T(8,128)(2,1)}, bf16[4,128,768]{...) custom-call(s32[1,512]{1,0:T(1,128)} %bitcast.20, ...), custom_call_target="tpu_custom_call" | custom-call | tf_op jit(solution)/shard_map/step_kernel/pallas_call | solution.py:742
  211.8 28.9 %table_kernel.1 = (f32[1]{0:T(128)}, f32[12576,768]{1,0:T(8,128)}, f32[768,768]{1,0:T(8,128)}, f32[768,768]{1,0:T(8,128)}) custom-call(s32[8,512]{1,0:T(8,128)} %get-tuple-element.17.meta, f32[8,128]{1,0:T(8,128)} %get-tuple-element.18.loss_in, bf16[512,768]{1,0:T(8,128)(2,1)} %bitcast.14, bf16[512,768]{1,0:T(8,128)(2,1)} %bitcast.15, ...), custom_call_target="tpu_custom_call" | custom-call | tf_op jit(solution)/shard_map/table_kernel/pallas_call | solution.py:767
